TPU v7x, 128 devices: a whole 4x4x4 slice. The times are simulated.
128 devices in a mesh: row: 8 (over z, core), col: 16 (over y, x).
Axes of the slice: x: 4, y: 4, z: 4, core: 2. Of those that a mesh axis runs over, the one named last changes fastest.
Arguments:
- coefs: float32 [2, 1536, 16384], P(None, 'row', 'col'), may hold values from -600 to 600, as said below
- tilts: int32 [1536, 2], replicated, may hold values from 8 to 48
- start_basis: float32 [1536, 32], P('col'), may hold values from -6 to 6
Outputs:
- ccc: float32 [1536, 1536], P('row', 'col')
- basis: float32 [1536, 32], P('col')
Inputs may be any that keep to these rules, and one draw needn't show every extreme that they name: `coefs`: real and imaginary parts are products of a particle scale, a coefficient scale and a bounded random value.
All inputs are finite; a program needn't handle non-finite values.
Results may differ from a plain program's by a relative error of at most 0.0003.
Values sent between devices are 32-bit elements; how exact they have to be, the bound alone decides.
A program may use at most 192 MiB of HBM per device.

v0:
```python
import math

import jax
import jax.numpy as jnp
from jax import lax
from jax.sharding import PartitionSpec as P

GRID = 32
ITERS = 4


EPS = 1e-06
HIGH = lax.Precision.HIGHEST


def in_blocks(array, dim, devices):
    before, after = (array.shape[:dim], array.shape[dim + 1 :])
    return jnp.moveaxis(array.reshape(*before, devices, -1, *after), dim, 0)


def sum_at_owner(array, axis, dim):
    tiles = in_blocks(array, dim, lax.axis_size(axis))
    arrived = lax.all_to_all(tiles, axis, split_axis=0, concat_axis=0, tiled=True)
    return arrived.sum(axis=0)


def from_everyone(array, axis):
    copies = jnp.broadcast_to(array, (lax.axis_size(axis), *array.shape))
    return lax.all_to_all(copies, axis, split_axis=0, concat_axis=0, tiled=True)


def over_copies(array, axis):
    return from_everyone(array, axis).sum(axis=0)


def laid_out(tiles, dim):
    dims = list(tiles.shape[1:])
    dims[dim] *= tiles.shape[0]
    return jnp.moveaxis(tiles, 0, dim).reshape(dims)


def gather_directly(array, axis, dim):
    return laid_out(from_everyone(array, axis), dim)


def wedge(tilt_rows, wave_index):
    wave_x = jnp.abs(wave_index // (GRID * (GRID // 2)) - GRID // 2)[None, :]
    wave_z = (wave_index % GRID - GRID // 2)[None, :]
    upward = wave_z * 16 <= tilt_rows[:, 1:2] * wave_x
    downward = -wave_z * 16 <= tilt_rows[:, 0:1] * wave_x
    return jnp.where(wave_z >= 0, upward, downward).astype(jnp.float32)


def inner(left, right):
    return lax.dot_general(
        left, right, (((1,), (1,)), ((), ())), precision=HIGH, preferred_element_type=jnp.float32
    )


def prepare(values, tilt_rows, wave_index):
    masks = wedge(tilt_rows, wave_index)
    paired = jnp.concatenate([values[0] * masks, values[1] * masks], axis=1)
    energy = masks * (values[0] * values[0] + values[1] * values[1])
    return (masks, paired, energy)


def local(coefs, tilts, start_basis):
    row_count = coefs.shape[1]
    slice_width = coefs.shape[2]
    col_count = start_basis.shape[0]
    col_size = lax.axis_size("col")
    total = col_count * col_size
    row_index = lax.axis_index("row")
    col_index = lax.axis_index("col")
    own_tilts = lax.dynamic_slice_in_dim(tilts, row_index * row_count, row_count, 0)
    wave_index = col_index * slice_width + jnp.arange(slice_width, dtype=jnp.int32)
    own_mask, own_pair, own_energy = prepare(coefs, own_tilts, wave_index)
    gathered = lax.all_gather(coefs, "row", axis=1, tiled=True)
    mask_j, pair_j, energy_j = prepare(gathered, tilts, wave_index)
    numer = inner(pair_j, own_pair)
    first = inner(mask_j, own_energy)
    second = inner(energy_j, own_mask)
    summed = sum_at_owner(jnp.concatenate([numer, first, second], axis=1), "col", 0)
    numer = summed[:, :row_count]
    first = summed[:, row_count : 2 * row_count]
    second = summed[:, 2 * row_count :]
    block = (numer / jnp.sqrt(first * second + EPS)).T
    current = start_basis
    for step in range(ITERS):
        partial_value = jnp.dot(block, current, precision=HIGH, preferred_element_type=jnp.float32)
        summed_rows = over_copies(partial_value, "col")
        local_gram = lax.dot_general(
            summed_rows,
            summed_rows,
            (((0,), (0,)), ((), ())),
            precision=HIGH,
            preferred_element_type=jnp.float32,
        )
        gram = over_copies(local_gram, "row")
        factor = jnp.linalg.cholesky(gram)
        fresh = lax.linalg.triangular_solve(
            factor, summed_rows, left_side=False, lower=True, transpose_a=True
        )
        whole = gather_directly(fresh, "row", 0)
        current = lax.dynamic_slice_in_dim(whole, col_index * col_count, col_count, 0)
    return (block, current * math.sqrt(total))


def solution(mesh):
    in_specs = (P(None, "row", "col"), P(), P("col", None))
    out_specs = (P("row", "col"), P("col", None))
    return jax.shard_map(local, mesh=mesh, in_specs=in_specs, out_specs=out_specs, check_vma=False)
```

profile of v0, /device:TPU:1, one launch (start us, length us, event | category | flops | bytes accessed | tf_op | source)
XLA Modules:
  0.0 345.3 jit_solution(13841363534144779767)
XLA Ops:
  7.9 0.8 fusion.70
  9.6 2.9 bitcast_select_fusion.1
  12.5 7.3 %fusion.18 = f32[1536,192]{0,1:T(8,128)} fusion(f32[2,192,1024]{2,1,0:T(8,128)} %param.6, s32[192]{0:T(256)S(1)} %bitcast.109, s32[1024]{0:T(1024)S(1)} %get-tuple-element.21, s32[1024]{0:T(1024)S(1)} %get-tuple-element.20, s32[192]{0:T(256)S(1)} %bitcast.106, s32[1024]{0:T(1024)S(1)} %broadcast_multiply_fusion, ...), kind=kOutput, calls=%fused_computation.29 | convolution fusion | flops 3633512448 | bytes 2797568 | tf_op jit(solution)/shard_map/dot_general | solution.py:55
  19.8 61.0 %all-gather.2.cloned.1.call-done = f32[2,1536,1024]{2,1,0:T(8,128)} async-done(((f32[2,192,1024]{2,1,0:T(8,128)}), f32[2,1536,1024]{2,1,0:T(8,128)}) %all-gather.2.cloned.1.call-update) | async-done | bytes 12582928 | tf_op jit(solution)/shard_map/all_gather | solution.py:78
  80.8 7.4 %fusion.10 = (f32[1536,1024]{1,0:T(8,128)S(1)}, f32[1536,1024]{1,0:T(8,128)S(1)}) fusion(f32[2,1536,1024]{2,1,0:T(8,128)} %all-gather.2.cloned.1.call-done, s32[1536]{0:T(1024)S(1)} %get-tuple-element.13, s32[1024]{0:T(1024)S(1)} %get-tuple-element.21, s32[1024]{0:T(1024)S(1)} %get-tuple-element.20, s32[1536]{0:T(1024)S(1)} %get-tuple-element.12, ...), kind=kLoop, calls=%fused_computation.14 | loop fusion | flops 11010048 | bytes 25191424 | tf_op jit(solution)/shard_map/mul | solution.py:62
  88.2 15.6 %fusion = f32[1536,192]{0,1:T(8,128)} fusion(f32[1536,1024]{1,0:T(8,128)S(1)} %get-tuple-element.15, f32[1536,1024]{1,0:T(8,128)S(1)} %get-tuple-element.14, f32[192,1024]{1,0:T(8,128)} %get-tuple-element.17, f32[192,1024]{1,0:T(8,128)} %get-tuple-element.16), kind=kOutput, calls=%fused_computation | convolution fusion | flops 7251296256 | bytes 15335424 | tf_op jit(solution)/shard_map/dot_general | solution.py:55
  103.9 6.2 %fusion.4 = f32[1536,192]{0,1:T(8,128)S(1)} fusion(f32[2,1536,1024]{2,1,0:T(8,128)S(1)} %bitcast.104, s32[192]{0:T(256)S(1)} %bitcast.110, s32[1024]{0:T(1024)S(1)} %get-tuple-element.21, s32[1024]{0:T(1024)S(1)} %get-tuple-element.20, s32[192]{0:T(256)S(1)} %bitcast.107, s32[1024]{0:T(1024)S(1)} %broadcast_multiply_fusion, ...), kind=kOutput, calls=%fused_computation.6 | convolution fusion | flops 3639017472 | bytes 13807616 | tf_op jit(solution)/shard_map/dot_general | solution.py:55
  110.4 3.1 copy.54
  113.5 54.3 %all_to_all.65 = f32[16,96,576]{2,1,0:T(8,128)} all-to-all(f32[16,96,576]{2,1,0:T(8,128)} %bitcast.102), channel_id=1, replica_groups=mesh['row'=8,'col'=16] {'col'}, dimensions={0} | all-to-all | bytes 7077888 | tf_op jit(solution)/shard_map/all_to_all | solution.py:23
  167.8 2.3 reduce_sum.81
  170.5 13.4 %all_to_all.66 = f32[16,192,32]{1,2,0:T(8,128)S(1)} all-to-all(f32[16,192,32]{1,2,0:T(8,128)S(1)} %broadcast_in_dim.59), channel_id=1, replica_groups=mesh['row'=8,'col'=16] {'col'}, dimensions={0} | all-to-all | bytes 786432 | tf_op jit(solution)/shard_map/all_to_all | solution.py:29
  184.3 10.0 %all_to_all.67 = f32[8,1,1024]{2,1,0:T(1,128)S(1)} all-to-all(f32[8,1,1024]{2,1,0:T(1,128)S(1)} %reshape.98), channel_id=1, replica_groups=mesh['row'=8,'col'=16] {'row'}, dimensions={0} | all-to-all | bytes 65536 | tf_op jit(solution)/shard_map/all_to_all | solution.py:29
  195.7 2.9 cholesky.74
  199.9 2.4 custom-call.8
  203.3 4.0 %all-to-all-start.3 = ((f32[8,192,32]{1,2,0:T(8,128)}), f32[8,192,32]{1,2,0:T(8,128)S(1)}, u32[]{:S(2)}, u32[]{:S(2)}) async-start(f32[8,192,32]{1,2,0:T(8,128)} %broadcast_in_dim.61), calls=%async_computation.3 | async-start | bytes 524288 | tf_op jit(solution)/shard_map/all_to_all | solution.py:29
  207.4 6.5 %all-to-all-done.3 = f32[8,192,32]{1,2,0:T(8,128)S(1)} async-done(((f32[8,192,32]{1,2,0:T(8,128)}), f32[8,192,32]{1,2,0:T(8,128)S(1)}, u32[]{:S(2)}, u32[]{:S(2)}) %all-to-all-start.3) | async-done | bytes 196640 | tf_op jit(solution)/shard_map/all_to_all | solution.py:29
  214.4 13.0 %all_to_all.68 = f32[16,192,32]{1,2,0:T(8,128)S(1)} all-to-all(f32[16,192,32]{1,2,0:T(8,128)S(1)} %broadcast_in_dim.62), channel_id=1, replica_groups=mesh['row'=8,'col'=16] {'col'}, dimensions={0} | all-to-all | bytes 786432 | tf_op jit(solution)/shard_map/all_to_all | solution.py:29
  227.8 9.2 %all_to_all.69 = f32[8,1,1024]{2,1,0:T(1,128)S(1)} all-to-all(f32[8,1,1024]{2,1,0:T(1,128)S(1)} %reshape.100), channel_id=1, replica_groups=mesh['row'=8,'col'=16] {'row'}, dimensions={0} | all-to-all | bytes 65536 | tf_op jit(solution)/shard_map/all_to_all | solution.py:29
  238.0 2.9 cholesky.85
  242.2 2.4 custom-call.9
  244.9 9.6 %all_to_all.70 = f32[8,192,32]{1,2,0:T(8,128)S(1)} all-to-all(f32[8,192,32]{1,2,0:T(8,128)S(1)} %broadcast_in_dim.64), channel_id=1, replica_groups=mesh['row'=8,'col'=16] {'row'}, dimensions={0} | all-to-all | bytes 393216 | tf_op jit(solution)/shard_map/all_to_all | solution.py:29
  255.1 13.0 %all_to_all.71 = f32[16,192,32]{1,2,0:T(8,128)S(1)} all-to-all(f32[16,192,32]{1,2,0:T(8,128)S(1)} %broadcast_in_dim.65), channel_id=1, replica_groups=mesh['row'=8,'col'=16] {'col'}, dimensions={0} | all-to-all | bytes 786432 | tf_op jit(solution)/shard_map/all_to_all | solution.py:29
  268.5 9.2 %all_to_all.72 = f32[8,1,1024]{2,1,0:T(1,128)S(1)} all-to-all(f32[8,1,1024]{2,1,0:T(1,128)S(1)} %reshape.102), channel_id=1, replica_groups=mesh['row'=8,'col'=16] {'row'}, dimensions={0} | all-to-all | bytes 65536 | tf_op jit(solution)/shard_map/all_to_all | solution.py:29
  278.6 2.9 cholesky.96
  282.9 2.4 custom-call.10
  285.6 9.6 %all_to_all.73 = f32[8,192,32]{1,2,0:T(8,128)S(1)} all-to-all(f32[8,192,32]{1,2,0:T(8,128)S(1)} %broadcast_in_dim.67), channel_id=1, replica_groups=mesh['row'=8,'col'=16] {'row'}, dimensions={0} | all-to-all | bytes 393216 | tf_op jit(solution)/shard_map/all_to_all | solution.py:29
  295.8 13.0 %all_to_all.74 = f32[16,192,32]{1,2,0:T(8,128)S(1)} all-to-all(f32[16,192,32]{1,2,0:T(8,128)S(1)} %broadcast_in_dim.68), channel_id=1, replica_groups=mesh['row'=8,'col'=16] {'col'}, dimensions={0} | all-to-all | bytes 786432 | tf_op jit(solution)/shard_map/all_to_all | solution.py:29
  309.2 9.2 %all_to_all.75 = f32[8,1,1024]{2,1,0:T(1,128)S(1)} all-to-all(f32[8,1,1024]{2,1,0:T(1,128)S(1)} %reshape.104), channel_id=1, replica_groups=mesh['row'=8,'col'=16] {'row'}, dimensions={0} | all-to-all | bytes 65536 | tf_op jit(solution)/shard_map/all_to_all | solution.py:29
  319.3 2.9 cholesky.107
  323.6 2.4 custom-call.11
  327.0 4.0 %all-to-all-start.12 = ((f32[8,192,32]{1,2,0:T(8,128)}), f32[8,192,32]{1,2,0:T(8,128)S(1)}, u32[]{:S(2)}, u32[]{:S(2)}) async-start(f32[8,192,32]{1,2,0:T(8,128)} %broadcast_in_dim.70), calls=%async_computation.12 | async-start | bytes 524288 | tf_op jit(solution)/shard_map/all_to_all | solution.py:29
  331.9 5.6 %all-to-all-done.12 = f32[8,192,32]{1,2,0:T(8,128)S(1)} async-done(((f32[8,192,32]{1,2,0:T(8,128)}), f32[8,192,32]{1,2,0:T(8,128)S(1)}, u32[]{:S(2)}, u32[]{:S(2)}) %all-to-all-start.12) | async-done | bytes 196640 | tf_op jit(solution)/shard_map/all_to_all | solution.py:29
  (97 shorter events, 18.8 us)
Async XLA Ops:
  7.2 163.1 %copy-start = (f32[96,32]{0,1:T(8,128)S(1)}, f32[96,32]{0,1:T(8,128)}, u32[]{:S(2)}) copy-start(f32[96,32]{0,1:T(8,128)} %param.8) | copy-start | bytes 36868
  7.2 73.6 %all-gather.2.cloned.1.call-start = ((), (), s32[]{:S(2)}) async-start(), calls=%async_computation.13 | async-start | bytes 14155776 | tf_op jit(solution)/shard_map/all_gather | solution.py:78
  80.8 23.1 %slice-start = ((s8[12582912]{0:T(1024)(128)(4,1)}), s8[4194304]{0:T(1024)(128)(4,1)S(1)}, s32[]{:S(2)}) async-start(s8[12582912]{0:T(1024)(128)(4,1)} %bitcast.103), calls=%async_computation.14 | async-start | bytes 8388608
  80.8 23.1 %slice-start.1 = ((s8[12582912]{0:T(1024)(128)(4,1)}), s8[4194304]{0:T(1024)(128)(4,1)S(1)}, s32[]{:S(2)}) async-start(s8[12582912]{0:T(1024)(128)(4,1)} %bitcast.103), calls=%async_computation.15 | async-start | bytes 8388608
  88.2 15.7 %slice-start.2 = ((s8[12582912]{0:T(1024)(128)(4,1)}), s8[4194304]{0:T(1024)(128)(4,1)S(1)}, s32[]{:S(2)}) async-start(s8[12582912]{0:T(1024)(128)(4,1)} %bitcast.103), calls=%async_computation.16 | async-start | bytes 8388608
  103.9 6.2 %copy-start.1 = (f32[1536,192]{0,1:T(8,128)S(1)}, f32[1536,192]{0,1:T(8,128)}, u32[]{:S(2)}) copy-start(f32[1536,192]{0,1:T(8,128)} %fusion) | copy-start | bytes 3538948
  103.9 6.2 %copy-start.2 = (f32[1536,192]{0,1:T(8,128)S(1)}, f32[1536,192]{0,1:T(8,128)}, u32[]{:S(2)}) copy-start(f32[1536,192]{0,1:T(8,128)} %fusion.18) | copy-start | bytes 3538948
  203.3 10.5 %all-to-all-start.3 = ((f32[8,192,32]{1,2,0:T(8,128)}), f32[8,192,32]{1,2,0:T(8,128)S(1)}, u32[]{:S(2)}, u32[]{:S(2)}) async-start(f32[8,192,32]{1,2,0:T(8,128)} %broadcast_in_dim.61), calls=%async_computation.3 | async-start | bytes 524288 | tf_op jit(solution)/shard_map/all_to_all | solution.py:29
  327.0 10.5 %all-to-all-start.12 = ((f32[8,192,32]{1,2,0:T(8,128)}), f32[8,192,32]{1,2,0:T(8,128)S(1)}, u32[]{:S(2)}, u32[]{:S(2)}) async-start(f32[8,192,32]{1,2,0:T(8,128)} %broadcast_in_dim.70), calls=%async_computation.12 | async-start | bytes 524288 | tf_op jit(solution)/shard_map/all_to_all | solution.py:29
Sparse Core Ops, SparseCore 0:
  9.7 71.0 all-gather.1
where the time goes:
time: 346 us; the launch traced here: 345 us
  blocking collectives  164 us (47%)
  waiting for transfers between devices  73.8 us (21%)
  other arithmetic  43.6 us (13%)
  matrix products  31.7 us (9%)
  between operations  14.5 us (4%)
  local copies, waits for them, and re-layouts  9.96 us (3%)
  starting transfers between devices  8.13 us (2%)
    all_to_all x10, blocking collectives, from_everyone(): return lax.all_to_all(copies, axis, split_axis=0, concat_axis=0, tiled=True)  109 us
    all_gather x1, waiting for transfers between devices, local(): gathered = lax.all_gather(coefs, 'row', axis=1, tiled=True)  61 us
    all_to_all x1, blocking collectives, sum_at_owner(): lax.all_to_all(tiles, axis, split_axis=0, concat_axis=0, tiled=True)  54.3 us
    dot_general x3, matrix products, inner(): lax.dot_general(left, right, (((1,), (1,)), ((), ())), precision=HIGH, pr...  29.2 us
    another operation x12, other arithmetic, local(): factor = jnp.linalg.cholesky(gram)  14.4 us
    another operation x8, other arithmetic, local(): lax.linalg.triangular_solve(factor, summed_rows, left_side=False, lower=T...  12.3 us
    all_to_all x2, waiting for transfers between devices, from_everyone(): return lax.all_to_all(copies, axis, split_axis=0, concat_axis=0, tiled=True)  12.1 us
    mul x2, other arithmetic, prepare(): paired = jnp.concatenate([values[0] * masks, values[1] * masks], axis=1)  10.3 us
  transfers between devices with their start and end apart: 3, of which 3 were waited for; matrix products, arithmetic and copies ran while one was open for 4% of the time, Pallas kernels for 0%

commit v1 on v0

v1 whole, which is shorter than its diff:
```python
import math

import jax
import jax.numpy as jnp
from jax import lax
from jax.experimental import pallas as pl
from jax.experimental.pallas import tpu as pltpu
from jax.sharding import PartitionSpec as P

GRID = 32
ITERS = 4
EPS = 1e-06
MESH = pl.DeviceIdType.MESH
F32 = jnp.float32
BF16 = jnp.bfloat16

ROWS = 192
LANES = 128
BLOCKS = 4
BLOCK = 384
PAIRS = [(a, b) for b in range(BLOCKS) for a in range(b + 1)]
TILES = 32
STACK = TILES * ROWS
COLOR = STACK // 3
SEGS = (COLOR // 4, COLOR // 16, COLOR // 64)
ORDERS = (("x", "y", "z"), ("y", "z", "x"), ("z", "x", "y"))
LOW = 8


def nt(left, right):
    return lax.dot_general(left, right, (((1,), (1,)), ((), ())), preferred_element_type=F32)


def nn(left, right):
    return lax.dot_general(left, right, (((1,), (0,)), ((), ())), preferred_element_type=F32)


def split(value):
    high = value.astype(BF16)
    return high, (value - high.astype(F32)).astype(BF16)


def kernel(
    coefs, tilts, start,
    rows_out, basis_out,
    sendbuf, own, other, x_high, x_low,
    partial, recv1, recv2, recv3, acc1, acc2, full, rden,
    table_x, table_y, table, lookup, lookup_in, first,
    c_high, c_low, vt,
    a2a_s, a2a_r, fwd_s, fwd_r, tab_s, tab_r, tf_s, tf_r, st_s, st_r,
    rs_s, rs_r, ag_s, ag_r, out_s, out_r,
):
    r = lax.axis_index("row")
    c = lax.axis_index("col")
    core = r % 2
    place = {"x": c % 4, "y": c // 4, "z": r // 2}

    def peer(axis, d):
        p = (place[axis] + d) % 4
        if axis == "x":
            return p, (r, place["y"] * 4 + p)
        if axis == "y":
            return p, (r, p * 4 + place["x"])
        return p, (p * 2 + core, c)

    partner = (place["z"] * 2 + 1 - core, c)

    def send(src, dst, ss, rs, device):
        copy = pltpu.make_async_remote_copy(
            src_ref=src, dst_ref=dst, send_sem=ss, recv_sem=rs,
            device_id=device, device_id_type=MESH,
        )
        copy.start()
        return copy

    barrier = pltpu.get_barrier_semaphore()
    for d in range(1, 8):
        pl.semaphore_signal(barrier, inc=1, device_id=((r + d) % 8, c), device_id_type=MESH)
    for axis in ("x", "y"):
        for d in range(1, 4):
            pl.semaphore_signal(barrier, inc=1, device_id=peer(axis, d)[1], device_id_type=MESH)

    mine = tilts[pl.ds(pl.multiple_of(r * ROWS, 8), ROWS), :]
    wave = c * 1024 + lax.broadcasted_iota(jnp.int32, (1, 1024), 1)
    wave_x = jnp.abs(wave // (GRID * (GRID // 2)) - GRID // 2)
    wave_z = wave % GRID - GRID // 2
    need = jnp.abs(wave_z) * 16
    limit = jnp.where(wave_z >= 0, mine[:, 1:2], mine[:, 0:1])
    masks = (need <= limit * wave_x).astype(F32)
    real = coefs[0] * masks
    imag = coefs[1] * masks
    for q in range(8):
        sendbuf[q, 0] = real[:, q * LANES : (q + 1) * LANES]
        sendbuf[q, 1] = imag[:, q * LANES : (q + 1) * LANES]
    own[r] = sendbuf[r]
    first[pl.ds(pl.multiple_of(c * 96, 8), 96), :] = jnp.zeros((96, LANES), F32)
    first[pl.ds(pl.multiple_of(c * 96, 8), 96), 0:32] = start[...]
    pl.semaphore_wait(barrier, 13)

    exchange = []
    for n, d in enumerate((2, 6, 1, 7, 3, 5, 4)):
        p = (r + d) % 8
        exchange.append((d, send(sendbuf.at[p], own.at[r], a2a_s.at[n], a2a_r.at[n], (p, c))))
    forward = [send(own.at[r], other.at[r], fwd_s.at[0], fwd_r.at[0], partner)]

    energy = real * real + imag * imag
    slope = lax.broadcasted_iota(jnp.int32, (LANES, 1), 0)
    side = jnp.where(slope < 64, 1, 0)
    below = need <= (slope % 64 + LOW) * wave_x
    positive = jnp.where(wave_z >= 0, 1, 0)
    pattern = jnp.where(below & (side == positive), 1.0, 0.0).astype(BF16)
    high, rest = split(energy)
    rest32 = energy - high.astype(F32)
    middle, low = split(rest32)
    sums = nt(high, pattern) + nt(middle, pattern) + nt(low, pattern)

    def ring_sum(buffer, value, axis, base):
        buffer[place[axis]] = value
        copies = []
        for d in range(1, 4):
            copies.append(send(
                buffer.at[place[axis]], buffer.at[place[axis]],
                tab_s.at[base + d - 1], tab_r.at[base + d - 1], peer(axis, d)[1],
            ))
        return copies

    copies = ring_sum(table_x, sums, "x", 0)
    mine_rows = pl.ds(pl.multiple_of(c * 96, 8), 96)
    starts = [
        send(first.at[mine_rows], first.at[mine_rows], st_s.at[d - 1], st_r.at[d - 1], peer("x", d)[1])
        for d in range(1, 4)
    ]
    column = lax.broadcasted_iota(jnp.int32, (1536, LANES), 1)
    chosen = (column == tilts[:, 1:2] - LOW) | (column == tilts[:, 0:1] - LOW + 64)
    chosen = jnp.where(chosen, 1.0, 0.0).astype(BF16)
    lookup[:, 0:LANES] = chosen
    lookup[:, LANES:] = chosen
    for copy in copies:
        copy.wait()
    total = (table_x[0] + table_x[1]) + (table_x[2] + table_x[3])
    copies = ring_sum(table_y, total, "y", 3)
    for copy in starts:
        copy.wait()
    mine_rows = pl.ds(pl.multiple_of(place["y"] * 384, 8), 384)
    starts = [
        send(first.at[mine_rows], first.at[mine_rows], st_s.at[d + 2], st_r.at[d + 2], peer("y", d)[1])
        for d in range(1, 4)
    ]
    for copy in copies:
        copy.wait()
    total = (table_y[0] + table_y[1]) + (table_y[2] + table_y[3])
    table[r] = total
    copies = [
        send(table.at[r], table.at[r], tab_s.at[5 + d], tab_r.at[5 + d], peer("z", d)[1])
        for d in range(1, 4)
    ]
    table_forward = [send(table.at[r], table.at[r], tf_s.at[0], tf_r.at[0], partner)]
    for copy in starts:
        copy.wait()

    for n, (d, copy) in enumerate(exchange):
        copy.wait()
        source = (r - d + 8) % 8
        forward.append(send(own.at[source], other.at[source], fwd_s.at[n + 1], fwd_r.at[n + 1], partner))
    for copy in forward:
        copy.wait()
    for source in range(8):
        for part, ref in enumerate((own, other)):
            for k in range(2):
                at = (2 * part + k) * LANES
                high, low = split(ref[source, k])
                x_high[source * ROWS : (source + 1) * ROWS, at : at + LANES] = high
                x_low[source * ROWS : (source + 1) * ROWS, at : at + LANES] = low

    reduce = {}

    def scatter(color, phase, source):
        axis = ORDERS[color][phase]
        size = SEGS[phase]
        target = (recv1, recv2, recv3)[phase]
        copies = []
        for d in range(1, 4):
            p, device = peer(axis, d)
            n = (color * 3 + phase) * 3 + d - 1
            copies.append(send(
                source.at[pl.ds(pl.multiple_of(p * size, 8), size)],
                target.at[color, d - 1], rs_s.at[n], rs_r.at[n], device,
            ))
        reduce[color, phase] = copies

    def gather_sum(color, phase, source):
        for copy in reduce[color, phase]:
            copy.wait()
        size = SEGS[phase]
        target = (recv1, recv2, recv3)[phase]
        at = place[ORDERS[color][phase]] * size
        value = source[pl.ds(pl.multiple_of(at, 8), size), :]
        return (value + target[color, 0]) + (target[color, 1] + target[color, 2])

    partial[30 * ROWS :, :] = jnp.zeros((2 * ROWS, LANES), F32)
    pair = 0
    begun = 0
    for b in range(BLOCKS):
        right_high = x_high[b * BLOCK : (b + 1) * BLOCK, :]
        right_low = x_low[b * BLOCK : (b + 1) * BLOCK, :]
        picks = [pl.ds(pl.multiple_of(a * BLOCK + core * ROWS, 8), ROWS) for a in range(b + 1)]
        left_high = jnp.concatenate([x_high[pick, :] for pick in picks], axis=0)
        left_low = jnp.concatenate([x_low[pick, :] for pick in picks], axis=0)
        product = nt(left_high, right_high) + nt(left_high, right_low) + nt(left_low, right_high)
        for a in range(b + 1):
            for k in range(3):
                at = (3 * pair + k) * ROWS
                partial[at : at + ROWS, :] = product[a * ROWS : (a + 1) * ROWS, k * LANES : (k + 1) * LANES]
            pair += 1
        done = pair * 3 * ROWS if b < BLOCKS - 1 else STACK
        while begun < 3 and (begun + 1) * COLOR <= done:
            scatter(begun, 0, partial.at[begun * COLOR : (begun + 1) * COLOR])
            begun += 1

    for d, copy in zip(range(1, 4), copies):
        copy.wait()
        source = ((place["z"] - d + 4) % 4) * 2 + core
        table_forward.append(send(table.at[source], table.at[source], tf_s.at[d], tf_r.at[d], partner))
    for copy in table_forward:
        copy.wait()
    for source in range(8):
        high, low = split(table[source])
        lookup_in[source * ROWS : (source + 1) * ROWS, 0:LANES] = high
        lookup_in[source * ROWS : (source + 1) * ROWS, LANES:] = low

    def norms(pair, a, b):
        def body(half, carry):
            pick = pl.ds(pl.multiple_of(a * BLOCK + half * ROWS, 8), ROWS)
            one = nt(lookup_in[pick, :], lookup[b * BLOCK : (b + 1) * BLOCK, :])
            two = nt(lookup[pick, :], lookup_in[b * BLOCK : (b + 1) * BLOCK, :])
            value = lax.rsqrt(one * two + EPS)
            for k in range(3):
                at = (3 * pair + k) * ROWS
                rden[half, at : at + ROWS, :] = value[:, k * LANES : (k + 1) * LANES]
            return carry

        lax.fori_loop(0, 2, body, 0)

    for pair, (a, b) in enumerate(PAIRS):
        norms(pair, a, b)

    for color in range(3):
        acc1[color] = gather_sum(color, 0, partial.at[color * COLOR : (color + 1) * COLOR])
        scatter(color, 1, acc1.at[color])
    for color in range(3):
        acc2[color] = gather_sum(color, 1, acc1.at[color])
        scatter(color, 2, acc2.at[color])

    spread = {}

    def region(color, phase):
        order = ORDERS[color]
        at = color * COLOR
        for step in range(phase + 1):
            at = at + place[order[step]] * SEGS[step]
        return at

    def broadcast(color, phase):
        piece = full.at[core, pl.ds(pl.multiple_of(region(color, phase), 8), SEGS[phase])]
        copies = []
        for d in range(1, 4):
            n = (color * 3 + phase) * 3 + d - 1
            copies.append(send(piece, piece, ag_s.at[n], ag_r.at[n], peer(ORDERS[color][phase], d)[1]))
        spread[color, phase] = copies

    for color in range(3):
        value = gather_sum(color, 2, acc2.at[color])
        full[core, pl.ds(pl.multiple_of(region(color, 2), 8), SEGS[2]), :] = value
        broadcast(color, 2)
    for phase in (1, 0):
        for color in range(3):
            for copy in spread[color, phase + 1]:
                copy.wait()
            broadcast(color, phase)
    last = []
    for color in range(3):
        for d in range(4):
            if d > 0:
                spread[color, 0][d - 1].wait()
            at = color * COLOR + ((place[ORDERS[color][0]] - d + 4) % 4) * SEGS[0]
            piece = full.at[core, pl.ds(pl.multiple_of(at, 8), SEGS[0])]
            n = color * 4 + d
            last.append(send(piece, piece, out_s.at[n], out_r.at[n], partner))
    for copy in last:
        copy.wait()

    for pair, (a, b) in enumerate(PAIRS):
        for k in range(3):
            at = (3 * pair + k) * ROWS
            halves = [full[half, at : at + ROWS, :] * rden[half, at : at + ROWS, :] for half in range(2)]
            value = jnp.concatenate(halves, axis=0)
            lane = b * BLOCK + k * LANES
            high, low = split(value)
            c_high[a * BLOCK : (a + 1) * BLOCK, lane : lane + LANES] = high
            c_low[a * BLOCK : (a + 1) * BLOCK, lane : lane + LANES] = low
            if a < b:
                high, low = split(value.T)
                c_high[lane : lane + LANES, a * BLOCK : (a + 1) * BLOCK] = high
                c_low[lane : lane + LANES, a * BLOCK : (a + 1) * BLOCK] = low
    pick = pl.ds(pl.multiple_of(r * ROWS, 16), ROWS)
    rows_out[...] = c_high[pick, :].astype(F32) + c_low[pick, :].astype(F32)

    vt[...] = first[...].T[0:32, :]
    row_of = lax.broadcasted_iota(jnp.int32, (32, 32), 0)
    column_of = lax.broadcasted_iota(jnp.int32, (32, 32), 1)

    def iterate(step, carry):
        v_high, v_low = split(vt[...])
        both = jnp.concatenate([v_high, v_low], axis=0)
        wide = nn(both, c_high[...])
        wide = wide[0:32] + wide[32:64] + nn(v_high, c_low[...])
        w_high, w_low = split(wide)
        gram = nt(w_high, w_high) + (nt(w_high, w_low) + nt(w_low, w_high))
        inverse = jnp.where(row_of == column_of, 1.0, 0.0).astype(F32)
        for j in range(32):
            factor = gram[:, j : j + 1] * (1.0 / gram[j : j + 1, j : j + 1])
            factor = jnp.where(row_of[:, 0:1] > j, factor, 0.0)
            gram, inverse = (
                gram - factor * gram[j : j + 1, :],
                inverse - factor * inverse[j : j + 1, :],
            )
        pivots = jnp.sum(jnp.where(row_of == column_of, gram, 0.0), axis=1, keepdims=True)
        inverse = inverse * lax.rsqrt(pivots)
        i_high, i_low = split(inverse)
        vt[...] = nn(i_high, w_high) + (nn(i_high, w_low) + nn(i_low, w_high))
        return carry

    lax.fori_loop(0, ITERS, iterate, 0)
    basis_out[...] = vt[...] * math.sqrt(1536)


def local(coefs, tilts, start_basis):
    vmem = pl.BlockSpec(memory_space=pltpu.VMEM)
    dma = pltpu.SemaphoreType.DMA
    rows, basis = pl.pallas_call(
        kernel,
        out_shape=(
            jax.ShapeDtypeStruct((ROWS, 1536), F32),
            jax.ShapeDtypeStruct((32, 1536), F32),
        ),
        in_specs=[vmem] * 3,
        out_specs=(vmem, vmem),
        scratch_shapes=[
            pltpu.VMEM((8, 2, ROWS, LANES), F32),
            pltpu.VMEM((8, 2, ROWS, LANES), F32),
            pltpu.VMEM((8, 2, ROWS, LANES), F32),
            pltpu.VMEM((1536, 512), BF16),
            pltpu.VMEM((1536, 512), BF16),
            pltpu.VMEM((STACK, LANES), F32),
            pltpu.VMEM((3, 3, SEGS[0], LANES), F32),
            pltpu.VMEM((3, 3, SEGS[1], LANES), F32),
            pltpu.VMEM((3, 3, SEGS[2], LANES), F32),
            pltpu.VMEM((3, SEGS[0], LANES), F32),
            pltpu.VMEM((3, SEGS[1], LANES), F32),
            pltpu.VMEM((2, STACK, LANES), F32),
            pltpu.VMEM((2, STACK, LANES), F32),
            pltpu.VMEM((4, ROWS, LANES), F32),
            pltpu.VMEM((4, ROWS, LANES), F32),
            pltpu.VMEM((8, ROWS, LANES), F32),
            pltpu.VMEM((1536, 2 * LANES), BF16),
            pltpu.VMEM((1536, 2 * LANES), BF16),
            pltpu.VMEM((1536, LANES), F32),
            pltpu.VMEM((1536, 1536), BF16),
            pltpu.VMEM((1536, 1536), BF16),
            pltpu.VMEM((32, 1536), F32),
            dma((7,)), dma((7,)), dma((8,)), dma((8,)),
            dma((9,)), dma((9,)), dma((4,)), dma((4,)), dma((6,)), dma((6,)),
            dma((27,)), dma((27,)), dma((27,)), dma((27,)), dma((12,)), dma((12,)),
        ],
        compiler_params=pltpu.CompilerParams(
            collective_id=0, has_side_effects=True, vmem_limit_bytes=62 << 20
        ),
        name="whole",
    )(coefs, tilts, start_basis)
    col = lax.axis_index("col")
    block = lax.dynamic_slice_in_dim(rows, col * 96, 96, 1)
    current = lax.dynamic_slice_in_dim(basis, col * 96, 96, 1).T
    return block, current


def solution(mesh):
    in_specs = (P(None, "row", "col"), P(), P("col", None))
    out_specs = (P("row", "col"), P("col", None))
    return jax.shard_map(local, mesh=mesh, in_specs=in_specs, out_specs=out_specs, check_vma=False)
```

time: 346 us -> 117 us (0.34)
  blocking collectives: 164 us -> 0 us
  Pallas kernels: 0 us -> 110 us
  waiting for transfers between devices: 73.8 us -> 0 us
  other arithmetic: 43.6 us -> 0 us
  matrix products: 31.7 us -> 0 us
  between operations: 14.5 us -> 0.64 us
  starting transfers between devices: 8.13 us -> 0 us
  local copies, waits for them, and re-layouts: 9.96 us -> 6.45 us
    all_to_all x11 -> x0, blocking collectives: 164 us -> none  [the longest x10 109 us: from_everyone(): return lax.all_to_all(copies, axis, split_axis=0, concat_axis=0, tiled=True)]
    pallas_call x0 -> x1, Pallas kernels: none -> 110 us  [local(): pl.pallas_call(kernel, out_shape=(jax.ShapeDtypeStruct((ROWS, 1536), F32)...]
    all_gather x1 -> x0, waiting for transfers between devices: 61 us -> none  [local(): gathered = lax.all_gather(coefs, 'row', axis=1, tiled=True)]
    dot_general x11 -> x0, matrix products: 30.7 us -> none  [the longest x3 29.2 us: inner(): lax.dot_general(left, right, (((1,), (1,)), ((), ())), precision=HIGH, pr...]
    another operation x20 -> x0, other arithmetic: 26.7 us -> none  [the longest x12 14.4 us: local(): factor = jnp.linalg.cholesky(gram)]
    all_to_all x2 -> x0, waiting for transfers between devices: 12.1 us -> none  [from_everyone(): return lax.all_to_all(copies, axis, split_axis=0, concat_axis=0, tiled=True)]
    mul x4 -> x0, other arithmetic: 11 us -> none  [the longest x2 10.3 us: prepare(): paired = jnp.concatenate([values[0] * masks, values[1] * masks], axis=1)]
    all_to_all x2 -> x0, starting transfers between devices: 8.09 us -> none  [from_everyone(): return lax.all_to_all(copies, axis, split_axis=0, concat_axis=0, tiled=True)]
  transfers between devices with their start and end apart: 3 -> 0, of which waited for: 3 -> 0; matrix products, arithmetic and copies ran while one was open for 4% -> 0% of each run, Pallas kernels for 0% -> 0%
where the time goes in v1:
time: 117 us
  Pallas kernels  110 us (94%)
  local copies, waits for them, and re-layouts  6.45 us (6%)
    pallas_call x1, Pallas kernels, local(): pl.pallas_call(kernel, out_shape=(jax.ShapeDtypeStruct((ROWS, 1536), F32)...  110 us
    unnamed x2, local copies, waits for them, and re-layouts  3.35 us

profile of v1, /device:TPU:1, one launch (start us, length us, event | category | flops | bytes accessed | tf_op | source)
XLA Modules:
  0.0 117.0 jit_solution(14828199805284179423)
XLA Ops:
  0.6 1.9 %copy.5.tilts = s32[1536,2]{1,0:T(8,128)} copy(s32[1536,2]{0,1:T(2,128)} %param.4) | data formatting | bytes 24576 | tf_op args[1]
  2.6 1.4 %copy.6.start = f32[96,32]{1,0:T(8,128)} copy(f32[96,32]{0,1:T(8,128)} %param.5) | data formatting | bytes 24576 | tf_op args[2]
  4.0 110.0 %whole.1 = (f32[192,1536]{1,0:T(8,128)}, f32[32,1536]{1,0:T(8,128)}) custom-call(f32[2,192,1024]{2,1,0:T(8,128)} %coefs.1, s32[1536,2]{1,0:T(8,128)} %copy.5.tilts, f32[96,32]{1,0:T(8,128)} %copy.6.start), custom_call_target="tpu_custom_call" | custom-call | tf_op jit(solution)/shard_map/whole/pallas_call | solution.py:340
  113.9 1.7 %constant_dynamic-slice_fusion = f32[192,96]{1,0:T(8,128)} fusion(f32[192,1536]{1,0:T(8,128)} %get-tuple-element.4, s32[]{:T(128)S(6)} %select_n.4), kind=kLoop, calls=%fused_computation.1 | loop fusion | bytes 147460 | tf_op jit(solution)/shard_map/dynamic_slice | solution.py:381
  115.6 1.4 %dynamic-slice_bitcast_fusion = f32[96,32]{0,1:T(8,128)} fusion(f32[32,1536]{1,0:T(8,128)} %get-tuple-element.5, s32[]{:T(128)S(6)} %select_n.4), kind=kLoop, calls=%fused_computation | loop fusion | bytes 24580 | tf_op jit(solution)/shard_map/transpose | solution.py:382

commit v2 on v0

v2 whole, which is shorter than its diff:
```python
import math

import jax
import jax.numpy as jnp
from jax import lax
from jax.experimental import pallas as pl
from jax.experimental.pallas import tpu as pltpu
from jax.sharding import PartitionSpec as P

GRID = 32
ITERS = 4
EPS = 1e-06
MESH = pl.DeviceIdType.MESH
F32 = jnp.float32
BF16 = jnp.bfloat16

ROWS = 192
PART = 96
N = 128
LOW = 8
WIDE = 6

SLOTS = ([], [])
for J in range(WIDE - 1, -1, -1):
    for half in range(2):
        odd = (half + J) % 2
        SLOTS[half].extend((2 * i + odd, 2 * J + k) for i in range(J) for k in range(2))
        SLOTS[half].append((2 * J + odd, 2 * J + 1))
    if J % 2 == 0:
        SLOTS[0].append((2 * J, 2 * J))
        SLOTS[1].append((2 * J + 2, 2 * J + 2))
TILES = len(SLOTS[0])
ORDERS = (("x", "y", "z"), ("y", "z", "x"), ("z", "x", "y"))
STREAMS = [(7 * s, 7, ORDERS[s]) for s in range(3)] + [(21 + 6 * s, 6, ORDERS[s]) for s in range(3)]
MOST = 7
PANEL = 16


def nt(left, right):
    return lax.dot_general(left, right, (((1,), (1,)), ((), ())), preferred_element_type=F32)


def nn(left, right):
    return lax.dot_general(left, right, (((1,), (0,)), ((), ())), preferred_element_type=F32)


def split(value):
    high = value.astype(BF16)
    return high, (value - high.astype(F32)).astype(BF16)


def rows_at(at, size):
    return pl.ds(pl.multiple_of(at, 8), size)


def lower_inverse(gram):
    row_of = lax.broadcasted_iota(jnp.int32, (32, 32), 0)
    column_of = lax.broadcasted_iota(jnp.int32, (32, 32), 1)

    def everywhere(value):
        return jnp.broadcast_to(value, (32, 32))

    inverse = jnp.where(row_of == column_of, 1.0, 0.0).astype(F32)
    pivots = jnp.ones((32, 32), F32)
    for j in range(0, 32, PANEL):
        columns = [everywhere(gram[:, j + q : j + q + 1]) for q in range(PANEL)]
        for p in range(PANEL):
            at = slice(j + p, j + p + 1)
            pivot = everywhere(columns[p][at, :])
            pivots = jnp.where(row_of == j + p, pivot, pivots)
            factor = jnp.where(row_of > j + p, columns[p] * (1.0 / pivot), 0.0)
            for q in range(p + 1, PANEL):
                columns[q] = columns[q] - factor * everywhere(columns[q][at, :])
            gram = gram - factor * everywhere(gram[at, :])
            inverse = inverse - factor * everywhere(inverse[at, :])
    return inverse * lax.rsqrt(pivots)


def kernel(
    coefs, tilts, start,
    block_out, basis_out,
    held, own, other, x_high, x_low, masks, chosen, corner,
    partial, recv_a, recv_b, recv_c, acc, full, rden,
    table_x, table_y, table, lookup, lookup_in, first,
    c_high, c_low, wt,
    held_s, a2a_s, a2a_r, fwd_s, fwd_r, tab_s, tab_r, tf_s, tf_r, st_s, st_r,
    ra_s, ra_r, rb_s, rb_r, rc_s, rc_r, gb_s, gb_r, ga_s, ga_r, out_s, out_r,
):
    r = lax.axis_index("row")
    c = lax.axis_index("col")
    core = r % 2
    mate = r + 1 - 2 * core
    place = {"x": c % 4, "y": c // 4, "z": r // 2}

    def peer(axis, d):
        p = (place[axis] + d) % 4
        if axis == "x":
            return p, (r, place["y"] * 4 + p)
        if axis == "y":
            return p, (r, p * 4 + place["x"])
        return p, (p * 2 + core, c)

    partner = (mate, c)

    def send(src, dst, ss, rs, device):
        copy = pltpu.make_async_remote_copy(
            src_ref=src, dst_ref=dst, send_sem=ss, recv_sem=rs,
            device_id=device, device_id_type=MESH,
        )
        copy.start()
        return copy

    barrier = pltpu.get_barrier_semaphore()
    for d in range(1, 8):
        pl.semaphore_signal(barrier, inc=1, device_id=((r + d) % 8, c), device_id_type=MESH)
    for axis in ("x", "y"):
        for d in range(1, 4):
            pl.semaphore_signal(barrier, inc=1, device_id=peer(axis, d)[1], device_id_type=MESH)
    locals_ = [pltpu.make_async_copy(coefs, held, held_s.at[0])]
    mine = pl.ds(pl.multiple_of(r * N, N), N)
    locals_.append(pltpu.make_async_copy(coefs.at[:, :, mine], own.at[r], held_s.at[1]))
    for copy in locals_:
        copy.start()
    corner[...] = jnp.zeros((N, N), F32)
    corner[0:32, 0:PART] = start[...]
    first[rows_at(c * PART, PART), :] = corner[...].T[0:PART, :]
    pl.semaphore_wait(barrier, 13)

    exchange = ([], [])
    forward = ([], [])
    for part in range(2):
        for n, d in enumerate((2, 6, 1, 7, 3, 5, 4)):
            p = (r + d) % 8
            n = 7 * part + n
            exchange[part].append((d, send(
                coefs.at[part, :, pl.ds(pl.multiple_of(p * N, N), N)],
                own.at[r, part], a2a_s.at[n], a2a_r.at[n], (p, c),
            )))
        forward[part].append(send(
            coefs.at[part, :, mine], other.at[r, part], fwd_s.at[8 * part], fwd_r.at[8 * part], partner,
        ))
    own_rows = rows_at(c * PART, PART)
    starts = [
        send(first.at[own_rows], first.at[own_rows], st_s.at[d - 1], st_r.at[d - 1], peer("x", d)[1])
        for d in range(1, 4)
    ]

    low_side = tilts[0:1, :]
    high_side = tilts[1:2, :]
    line = lax.broadcasted_iota(jnp.int32, (N, 1536), 0)
    picked = (line == high_side - LOW) | (line == low_side - LOW + 64)
    picked = jnp.where(picked, 1.0, 0.0)
    picked = jnp.where(line == 126, low_side.astype(F32), picked)
    picked = jnp.where(line == 127, high_side.astype(F32), picked)
    chosen[...] = picked.T
    column = lax.broadcasted_iota(jnp.int32, (1536, N), 1)
    one_hot = jnp.where(column < 126, chosen[...], 0.0).astype(BF16)
    lookup[:, 0:N] = one_hot
    lookup[:, N:] = one_hot

    def waves(at, count):
        wave = at + lax.broadcasted_iota(jnp.int32, (1, count), 1)
        wave_x = jnp.abs(wave // (GRID * (GRID // 2)) - GRID // 2).astype(F32)
        wave_z = wave % GRID - GRID // 2
        return wave_x, wave_z >= 0, (jnp.abs(wave_z) * 16).astype(F32)

    def wedge(pick, wave):
        wave_x, upward, need = wave
        limit = jnp.where(upward, chosen[pick, 127:128], chosen[pick, 126:127])
        return jnp.where(need <= limit * wave_x, 1.0, 0.0)

    for side, position in enumerate((r, mate)):
        wave = waves(c * 1024 + position * N, N)
        for source in range(8):
            pick = pl.ds(source * ROWS, ROWS)
            masks[pick, side * N : (side + 1) * N] = wedge(pick, wave)

    wave = waves(c * 1024, 1024)
    wave_x, upward, need = wave
    own_mask = wedge(rows_at(r * ROWS, ROWS), wave)
    for copy in locals_:
        copy.wait()
    real, imag = held[0] * own_mask, held[1] * own_mask
    energy = real * real + imag * imag
    slope = lax.broadcasted_iota(jnp.int32, (N, 1), 0)
    below = need <= (slope % 64 + LOW).astype(F32) * wave_x
    side = jnp.where(slope < 64, 1, 0) == jnp.where(upward, 1, 0)
    pattern = jnp.where(below & side, 1.0, 0.0).astype(BF16)
    high = energy.astype(BF16)
    middle, low = split(energy - high.astype(F32))
    sums = nt(high, pattern) + nt(middle, pattern) + nt(low, pattern)

    def ring_send(buffer, value, axis, base):
        buffer[place[axis]] = value
        return [
            send(
                buffer.at[place[axis]], buffer.at[place[axis]],
                tab_s.at[base + d - 1], tab_r.at[base + d - 1], peer(axis, d)[1],
            )
            for d in range(1, 4)
        ]

    copies = ring_send(table_x, sums, "x", 0)
    for copy in starts:
        copy.wait()
    own_rows = rows_at(place["y"] * 4 * PART, 4 * PART)
    starts = [
        send(first.at[own_rows], first.at[own_rows], st_s.at[d + 2], st_r.at[d + 2], peer("y", d)[1])
        for d in range(1, 4)
    ]
    for copy in copies:
        copy.wait()
    copies = ring_send(table_y, (table_x[0] + table_x[1]) + (table_x[2] + table_x[3]), "y", 3)

    def arrive(part):
        for n, (d, copy) in enumerate(exchange[part]):
            copy.wait()
            source = (r - d + 8) % 8
            n = 8 * part + n + 1
            forward[part].append(send(
                own.at[source, part], other.at[source, part], fwd_s.at[n], fwd_r.at[n], partner,
            ))
        for side, ref in enumerate((own, other)):
            if side == 1:
                for copy in forward[part]:
                    copy.wait()
            for source in range(8):
                pick = pl.ds(source * ROWS, ROWS)
                lane = slice(side * N, (side + 1) * N)
                high, low = split(ref[source, part] * masks[pick, lane])
                x_high[part, pick, lane] = high
                x_low[part, pick, lane] = low

    started = {}

    def scatter(s, source, buffer, size, axis, ss, rs):
        copies = []
        for d in range(1, 4):
            p, device = peer(axis, d)
            n = 3 * s + d - 1
            copies.append(send(
                source.at[rows_at(p * size, size)],
                buffer.at[s, d - 1, pl.ds(0, size)], ss.at[n], rs.at[n], device,
            ))
        return copies

    def scatter_a(s):
        at, count, order = STREAMS[s]
        source = partial.at[pl.ds(at * N, count * N)]
        started["a", s] = scatter(s, source, recv_a, count * 32, order[0], ra_s, ra_r)

    def products(part):
        at = 0
        stream = 0
        extra = None
        for J in range(WIDE - 1, -1, -1):
            odd = (core + J) % 2
            right_high = x_high[part, J * 2 * N : (J + 1) * 2 * N, :]
            right_low = x_low[part, J * 2 * N : (J + 1) * 2 * N, :]
            picks = [pl.ds(pl.multiple_of((2 * i + odd) * N, N), N) for i in range(J + 1)]
            left_high = jnp.concatenate([x_high[part, pick, :] for pick in picks], axis=0)
            left_low = jnp.concatenate([x_low[part, pick, :] for pick in picks], axis=0)
            product = nt(left_high, right_high) + nt(left_high, right_low) + nt(left_low, right_high)
            tiles = [product[i * N : (i + 1) * N, k * N : (k + 1) * N] for i in range(J + 1) for k in range(2)]
            spare = tiles.pop(2 * J)
            if J % 2 == 1:
                extra = spare
            else:
                tiles.append(jnp.where(core == 0, spare, extra))
            for tile in tiles:
                pick = slice(at * N, (at + 1) * N)
                if part == 0:
                    partial[pick, :] = tile
                else:
                    partial[pick, :] += tile
                at += 1
            if part == 1:
                while stream < 6 and STREAMS[stream][0] + STREAMS[stream][1] <= at:
                    scatter_a(stream)
                    stream += 1

    arrive(0)
    products(0)
    for copy in copies:
        copy.wait()
    table[r] = (table_y[0] + table_y[1]) + (table_y[2] + table_y[3])
    copies = [
        send(table.at[r], table.at[r], tab_s.at[5 + d], tab_r.at[5 + d], peer("z", d)[1])
        for d in range(1, 4)
    ]
    table_forward = [send(table.at[r], table.at[r], tf_s.at[0], tf_r.at[0], partner)]
    for copy in starts:
        copy.wait()
    arrive(1)
    products(1)

    for d, copy in zip(range(1, 4), copies):
        copy.wait()
        source = ((place["z"] - d + 4) % 4) * 2 + core
        table_forward.append(send(table.at[source], table.at[source], tf_s.at[d], tf_r.at[d], partner))
    for copy in table_forward:
        copy.wait()
    for source in range(8):
        high, low = split(table[source])
        lookup_in[source * ROWS : (source + 1) * ROWS, 0:N] = high
        lookup_in[source * ROWS : (source + 1) * ROWS, N:] = low

    def norms(half):
        at = 0
        extra = None
        for J in range(WIDE - 1, -1, -1):
            odd = (half + J) % 2
            right = slice(J * 2 * N, (J + 1) * 2 * N)
            picks = [slice((2 * i + odd) * N, (2 * i + odd + 1) * N) for i in range(J + 1)]
            sums_in = jnp.concatenate([lookup_in[pick, :] for pick in picks], axis=0)
            select = jnp.concatenate([lookup[pick, :] for pick in picks], axis=0)
            value = lax.rsqrt(nt(sums_in, lookup[right, :]) * nt(select, lookup_in[right, :]) + EPS)
            tiles = [value[i * N : (i + 1) * N, k * N : (k + 1) * N] for i in range(J + 1) for k in range(2)]
            spare = tiles.pop(2 * J)
            if odd == 0:
                extra = spare
            if J % 2 == 0:
                tiles.append(extra)
            for tile in tiles:
                rden[half, at * N : (at + 1) * N, :] = tile
                at += 1

    for half in range(2):
        norms(half)

    def scatter_b(s):
        count, order = STREAMS[s][1:]
        size = count * 32
        for copy in started["a", s]:
            copy.wait()
        pick = rows_at(STREAMS[s][0] * N + place[order[0]] * size, size)
        got = [recv_a[s, n, 0:size, :] for n in range(3)]
        acc[s, 0:size, :] = (partial[pick, :] + got[0]) + (got[1] + got[2])
        started["b", s] = scatter(s, acc.at[s], recv_b, count * 8, order[1], rb_s, rb_r)

    def spread_c(s):
        count, order = STREAMS[s][1:]
        size = count * 8
        for copy in started["b", s]:
            copy.wait()
        got = [recv_b[s, n, 0:size, :] for n in range(3)]
        value = (acc[s, rows_at(place[order[1]] * size, size), :] + got[0]) + (got[1] + got[2])
        here = place[order[2]]
        recv_c[s, here, 0:size, :] = value
        piece = recv_c.at[s, here, pl.ds(0, size)]
        started["c", s] = [
            send(piece, piece, rc_s.at[3 * s + d - 1], rc_r.at[3 * s + d - 1], peer(order[2], d)[1])
            for d in range(1, 4)
        ]

    def gather_b(s):
        at, count, order = STREAMS[s]
        size = count * 8
        for copy in started["c", s]:
            copy.wait()
        got = [recv_c[s, n, 0:size, :] for n in range(4)]
        pick = rows_at(at * N + (place[order[0]] * 4 + place[order[1]]) * size, size)
        full[core, pick, :] = (got[0] + got[1]) + (got[2] + got[3])
        piece = full.at[core, pick]
        started["B", s] = [
            send(piece, piece, gb_s.at[3 * s + d - 1], gb_r.at[3 * s + d - 1], peer(order[1], d)[1])
            for d in range(1, 4)
        ]

    def pass_on(s, d, order, at, size):
        piece = full.at[core, rows_at(at * N + (place[order[0]] - d + 4) % 4 * size, size)]
        return send(piece, piece, out_s.at[4 * s + d], out_r.at[4 * s + d], partner)

    def gather_a(s):
        at, count, order = STREAMS[s]
        size = count * 32
        for copy in started["B", s]:
            copy.wait()
        piece = full.at[core, rows_at(at * N + place[order[0]] * size, size)]
        started["A", s] = [
            send(piece, piece, ga_s.at[3 * s + d - 1], ga_r.at[3 * s + d - 1], peer(order[0], d)[1])
            for d in range(1, 4)
        ]
        started["out", s] = [pass_on(s, 0, order, at, size)]

    def finish(s):
        at, count, order = STREAMS[s]
        for d in (1, 3, 2):
            started["A", s][d - 1].wait()
            started["out", s].append(pass_on(s, d, order, at, count * 32))

    def assemble(s):
        at, count, order = STREAMS[s]
        for copy in started["out", s]:
            copy.wait()
        for tile in range(at, at + count):
            for half in range(2):
                A, B = SLOTS[half][tile]
                pick = slice(tile * N, (tile + 1) * N)
                value = full[half, pick, :] * rden[half, pick, :]
                high, low = split(value)
                down, across = slice(A * N, (A + 1) * N), slice(B * N, (B + 1) * N)
                c_high[down, across] = high
                c_low[down, across] = low
                if A < B:
                    high, low = split(value.T)
                    c_high[across, down] = high
                    c_low[across, down] = low

    early, late = (0, 1, 2), (3, 4, 5)
    for s in early:
        scatter_b(s)
    for s in early:
        spread_c(s)
    for s in late:
        scatter_b(s)
    for s in early:
        gather_b(s)
    for s in late:
        spread_c(s)
    for s in early:
        gather_a(s)
    for s in late:
        gather_b(s)
    for s in late:
        gather_a(s)
    for s in early:
        finish(s)
    for s in early:
        assemble(s)
    for s in late:
        finish(s)
    for s in late:
        assemble(s)

    def times_matrix(high, low):
        wide = nn(jnp.concatenate([high, low], axis=0), c_high[...])
        return wide[0:32] + wide[32:64] + nn(high, c_low[...])

    def gram_of(high, low):
        return nt(high, high) + (nt(high, low) + nt(low, high))

    def solved(inverse, high, low):
        inverse_high, inverse_low = split(inverse)
        return nn(inverse_high, high) + (nn(inverse_high, low) + nn(inverse_low, high))

    wt[...] = first[...].T[0:32, :]

    def iterate(step, carry):
        high, low = split(times_matrix(*split(wt[...])))
        inverse = lower_inverse(gram_of(high, low))
        wt[...] = solved(inverse, high, low)
        return carry

    lax.fori_loop(0, ITERS, iterate, 0)
    first[:, 0:32] = (wt[...] * math.sqrt(1536)).T
    basis_out[...] = first[rows_at(c * PART, PART), :].T[0:32, :]
    lane = jnp.minimum(c * PART // N, 1536 // N - 2) * N
    window = pl.ds(pl.multiple_of(lane, N), 2 * N)
    pick = pl.ds(pl.multiple_of(r * ROWS, 16), ROWS)
    block = c_high[pick, window].astype(F32) + c_low[pick, window].astype(F32)
    block = pltpu.roll(block, (2 * N - (c * PART - lane)) % (2 * N), 1)
    block_out[...] = block[:, 0:PART]


def local(coefs, tilts, start_basis):
    vmem = pl.BlockSpec(memory_space=pltpu.VMEM)
    dma = pltpu.SemaphoreType.DMA
    block, basis = pl.pallas_call(
        kernel,
        out_shape=(
            jax.ShapeDtypeStruct((ROWS, PART), F32),
            jax.ShapeDtypeStruct((32, PART), F32),
        ),
        in_specs=[pl.BlockSpec(memory_space=pltpu.HBM), vmem, vmem],
        out_specs=(vmem, vmem),
        scratch_shapes=[
            pltpu.VMEM((2, ROWS, 1024), F32),
            pltpu.VMEM((8, 2, ROWS, N), F32),
            pltpu.VMEM((8, 2, ROWS, N), F32),
            pltpu.VMEM((2, 1536, 2 * N), BF16),
            pltpu.VMEM((2, 1536, 2 * N), BF16),
            pltpu.VMEM((1536, 2 * N), F32),
            pltpu.VMEM((1536, N), F32),
            pltpu.VMEM((N, N), F32),
            pltpu.VMEM((TILES * N, N), F32),
            pltpu.VMEM((6, 3, MOST * 32, N), F32),
            pltpu.VMEM((6, 3, MOST * 8, N), F32),
            pltpu.VMEM((6, 4, MOST * 8, N), F32),
            pltpu.VMEM((6, MOST * 32, N), F32),
            pltpu.VMEM((2, TILES * N, N), F32),
            pltpu.VMEM((2, TILES * N, N), F32),
            pltpu.VMEM((4, ROWS, N), F32),
            pltpu.VMEM((4, ROWS, N), F32),
            pltpu.VMEM((8, ROWS, N), F32),
            pltpu.VMEM((1536, 2 * N), BF16),
            pltpu.VMEM((1536, 2 * N), BF16),
            pltpu.VMEM((1536, N), F32),
            pltpu.VMEM((1536, 1536), BF16),
            pltpu.VMEM((1536, 1536), BF16),
            pltpu.VMEM((32, 1536), F32),
            dma((2,)),
            dma((14,)), dma((14,)), dma((16,)), dma((16,)),
            dma((9,)), dma((9,)), dma((4,)), dma((4,)), dma((6,)), dma((6,)),
            dma((18,)), dma((18,)), dma((18,)), dma((18,)), dma((18,)), dma((18,)),
            dma((18,)), dma((18,)), dma((18,)), dma((18,)), dma((24,)), dma((24,)),
        ],
        compiler_params=pltpu.CompilerParams(
            collective_id=0, has_side_effects=True, vmem_limit_bytes=54272 << 10
        ),
        name="whole",
    )(coefs, tilts.T, start_basis.T)
    return block, basis.T


def solution(mesh):
    in_specs = (P(None, "row", "col"), P(), P("col", None))
    out_specs = (P("row", "col"), P("col", None))
    return jax.shard_map(local, mesh=mesh, in_specs=in_specs, out_specs=out_specs, check_vma=False)
```

time: 346 us -> 85.3 us (0.25)
  blocking collectives: 164 us -> 0 us
  Pallas kernels: 0 us -> 81.8 us
  waiting for transfers between devices: 73.8 us -> 0 us
  other arithmetic: 43.6 us -> 0 us
  matrix products: 31.7 us -> 0 us
  between operations: 14.5 us -> 0.65 us
  starting transfers between devices: 8.13 us -> 0 us
  local copies, waits for them, and re-layouts: 9.96 us -> 2.66 us
    all_to_all x11 -> x0, blocking collectives: 164 us -> none  [the longest x10 109 us: from_everyone(): return lax.all_to_all(copies, axis, split_axis=0, concat_axis=0, tiled=True)]
    pallas_call x0 -> x1, Pallas kernels: none -> 81.8 us  [local(): pl.pallas_call(kernel, out_shape=(jax.ShapeDtypeStruct((ROWS, PART), F32)...]
    all_gather x1 -> x0, waiting for transfers between devices: 61 us -> none  [local(): gathered = lax.all_gather(coefs, 'row', axis=1, tiled=True)]
    dot_general x11 -> x0, matrix products: 30.7 us -> none  [the longest x3 29.2 us: inner(): lax.dot_general(left, right, (((1,), (1,)), ((), ())), precision=HIGH, pr...]
    another operation x20 -> x0, other arithmetic: 26.7 us -> none  [the longest x12 14.4 us: local(): factor = jnp.linalg.cholesky(gram)]
    all_to_all x2 -> x0, waiting for transfers between devices: 12.1 us -> none  [from_everyone(): return lax.all_to_all(copies, axis, split_axis=0, concat_axis=0, tiled=True)]
    mul x4 -> x0, other arithmetic: 11 us -> none  [the longest x2 10.3 us: prepare(): paired = jnp.concatenate([values[0] * masks, values[1] * masks], axis=1)]
    all_to_all x2 -> x0, starting transfers between devices: 8.09 us -> none  [from_everyone(): return lax.all_to_all(copies, axis, split_axis=0, concat_axis=0, tiled=True)]
  transfers between devices with their start and end apart: 3 -> 0, of which waited for: 3 -> 0; matrix products, arithmetic and copies ran while one was open for 4% -> 0% of each run, Pallas kernels for 0% -> 0%
where the time goes in v2:
time: 85.3 us; the launch traced here: 85.1 us
  Pallas kernels  81.8 us (96%)
  local copies, waits for them, and re-layouts  2.66 us (3%)
    pallas_call x1, Pallas kernels, local(): pl.pallas_call(kernel, out_shape=(jax.ShapeDtypeStruct((ROWS, PART), F32)...  81.8 us
    unnamed x6, local copies, waits for them, and re-layouts  2.66 us

profile of v2, /device:TPU:1, one launch (start us, length us, event | category | flops | bytes accessed | tf_op | source)
XLA Modules:
  0.0 85.1 jit_solution(16158865107871096349)
XLA Ops:
  0.6 0.0 copy-start
  0.6 0.7 copy-done
  1.3 0.0 copy-start.1
  1.4 0.7 copy-done.1
  2.1 81.8 %whole.1 = (f32[192,96]{1,0:T(8,128)S(1)}, f32[32,96]{1,0:T(8,128)S(1)}) custom-call(f32[2,192,1024]{2,1,0:T(8,128)} %coefs.1, s32[2,1536]{1,0:T(2,128)S(1)} %bitcast.5, f32[32,96]{1,0:T(8,128)S(1)} %bitcast.3), custom_call_target="tpu_custom_call" | custom-call | tf_op jit(solution)/shard_map/whole/pallas_call | solution.py:469
  83.9 0.6 copy.7
  84.5 0.6 copy.8
Async XLA Ops:
  0.6 0.7 copy-start
  1.3 0.7 copy-start.1

commit v3 on v2

v3 whole, which is shorter than its diff:
```python
import math

import jax
import jax.numpy as jnp
from jax import lax
from jax.experimental import pallas as pl
from jax.experimental.pallas import tpu as pltpu
from jax.sharding import PartitionSpec as P

GRID = 32
ITERS = 4
EPS = 1e-06
MESH = pl.DeviceIdType.MESH
F32 = jnp.float32
BF16 = jnp.bfloat16

ROWS = 192
PART = 96
N = 128
LOW = 8
WIDE = 6

HALF = 768

SLOTS = ([], [])
for wave in ((2, 1, 0), (5, 4, 3)):
    for J in wave:
        for half in range(2):
            odd = (half + J) % 2
            SLOTS[half].extend((2 * i + odd, 2 * J + k) for i in range(J) for k in range(2))
            SLOTS[half].append((2 * J + odd, 2 * J + 1))
        if J in (0, 4, 3):
            low = J - J % 2
            SLOTS[0].append((2 * low, 2 * low))
            SLOTS[1].append((2 * low + 2, 2 * low + 2))
PLACE = [{tile: n for n, tile in enumerate(slots)} for slots in SLOTS]
TILES = len(SLOTS[0])
ORDERS = (("x", "y", "z"), ("y", "x", "z"), ("z", "x", "y"))
STREAMS = [(0, 5, ("x", "y", "z")), (5, 5, ("y", "x", "z"))]
for counts in ((4, 3, 3), (3, 4, 3), (3, 3, 3)):
    for count, order in zip(counts, ORDERS):
        STREAMS.append((STREAMS[-1][0] + STREAMS[-1][1], count, order))
MOST = 5
RELAYED = (0, 1)
HELD_BACK = (7, 10)
PANEL = 16


def nt(left, right):
    return lax.dot_general(left, right, (((1,), (1,)), ((), ())), preferred_element_type=F32)


def nn(left, right):
    return lax.dot_general(left, right, (((1,), (0,)), ((), ())), preferred_element_type=F32)


def split(value):
    high = value.astype(BF16)
    return high, (value - high.astype(F32)).astype(BF16)


def rows_at(at, size):
    return pl.ds(pl.multiple_of(at, 8), size)


def lower_inverse(gram):
    row_of = lax.broadcasted_iota(jnp.int32, (32, 32), 0)
    column_of = lax.broadcasted_iota(jnp.int32, (32, 32), 1)

    def everywhere(value):
        return jnp.broadcast_to(value, (32, 32))

    inverse = jnp.where(row_of == column_of, 1.0, 0.0).astype(F32)
    pivots = jnp.ones((32, 32), F32)
    for j in range(0, 32, PANEL):
        columns = [everywhere(gram[:, j + q : j + q + 1]) for q in range(PANEL)]
        for p in range(PANEL):
            at = slice(j + p, j + p + 1)
            pivot = everywhere(columns[p][at, :])
            pivots = jnp.where(row_of == j + p, pivot, pivots)
            factor = jnp.where(row_of > j + p, columns[p] * (1.0 / pivot), 0.0)
            for q in range(p + 1, PANEL):
                columns[q] = columns[q] - factor * everywhere(columns[q][at, :])
            gram = gram - factor * everywhere(gram[at, :])
            inverse = inverse - factor * everywhere(inverse[at, :])
    return inverse * lax.rsqrt(pivots)


def kernel(
    coefs, tilts_in, start_in,
    block_out, basis_out,
    tilts, start, held, own, other, x_high, x_low, masks, chosen, corner,
    partial, recv_a, recv_b, recv_c, acc, full, rden,
    table_x, table_y, table, lookup, lookup_in, first,
    c_high, c_low, wt,
    held_s, a2a_s, a2a_r, fwd_s, fwd_r, tab_s, tab_r, tf_s, tf_r, st_s, st_r,
    ra_s, ra_r, rb_s, rb_r, rc_s, rc_r, gb_s, gb_r, ga_s, ga_r, out_s, out_r,
):
    r = lax.axis_index("row")
    c = lax.axis_index("col")
    core = r % 2
    mate = r + 1 - 2 * core
    place = {"x": c % 4, "y": c // 4, "z": r // 2}

    def peer(axis, d):
        p = (place[axis] + d) % 4
        if axis == "x":
            return p, (r, place["y"] * 4 + p)
        if axis == "y":
            return p, (r, p * 4 + place["x"])
        return p, (p * 2 + core, c)

    partner = (mate, c)

    def send(src, dst, ss, rs, device):
        copy = pltpu.make_async_remote_copy(
            src_ref=src, dst_ref=dst, send_sem=ss, recv_sem=rs,
            device_id=device, device_id_type=MESH,
        )
        copy.start()
        return copy

    barrier = pltpu.get_barrier_semaphore()
    for d in range(1, 8):
        pl.semaphore_signal(barrier, inc=1, device_id=((r + d) % 8, c), device_id_type=MESH)
    for axis in ("x", "y"):
        for d in range(1, 4):
            pl.semaphore_signal(barrier, inc=1, device_id=peer(axis, d)[1], device_id_type=MESH)
    held_copy = pltpu.make_async_copy(coefs, held, held_s.at[0])
    held_copy.start()
    small_copies = [
        pltpu.make_async_copy(start_in, start, held_s.at[1]),
        pltpu.make_async_copy(tilts_in, tilts, held_s.at[2]),
    ]
    for copy in small_copies:
        copy.start()
    mine = pl.ds(pl.multiple_of(r * N, N), N)
    corner[...] = jnp.zeros((N, N), F32)
    small_copies[0].wait()
    corner[0:32, 0:PART] = start[...]
    here = (c % 2 * 8 + c // 2) * PART
    first[rows_at(here, PART), :] = corner[...].T[0:PART, :]
    held_copy.wait()
    pl.semaphore_wait(barrier, 13)

    cuts = (
        (slice(0, 2), pl.ds(0, PART)),
        (slice(0, 1), pl.ds(PART, PART)),
        (slice(1, 2), pl.ds(PART, PART)),
    )
    exchange = ([], [], [])
    forward = ([], [], [])
    for step, (parts, rows) in enumerate(cuts):
        for n, d in enumerate((2, 6, 1, 7, 3, 5, 4)):
            p = (r + d) % 8
            n = 7 * step + n
            exchange[step].append((d, send(
                held.at[parts, rows, pl.ds(pl.multiple_of(p * N, N), N)],
                own.at[r, parts, rows], a2a_s.at[n], a2a_r.at[n], (p, c),
            )))
        forward[step].append(send(
            held.at[parts, rows, mine], other.at[r, parts, rows],
            fwd_s.at[8 * step], fwd_r.at[8 * step], partner,
        ))
    own_rows = rows_at(here, PART)
    starts = [
        send(first.at[own_rows], first.at[own_rows], st_s.at[d - 1], st_r.at[d - 1], peer("x", d)[1])
        for d in range(1, 4)
    ]

    small_copies[1].wait()
    low_side = tilts[0:1, :]
    high_side = tilts[1:2, :]
    line = lax.broadcasted_iota(jnp.int32, (N, 1536), 0)
    picked = (line == high_side - LOW) | (line == low_side - LOW + 64)
    picked = jnp.where(picked, 1.0, 0.0)
    picked = jnp.where(line == 126, low_side.astype(F32), picked)
    picked = jnp.where(line == 127, high_side.astype(F32), picked)
    picked = picked.T
    for n in range(16):
        at = (n % 2 * 8 + n // 2) * PART
        chosen[at : at + PART, :] = picked[n * PART : (n + 1) * PART, :]
    column = lax.broadcasted_iota(jnp.int32, (1536, N), 1)
    one_hot = jnp.where(column < 126, chosen[...], 0.0).astype(BF16)
    lookup[:, 0:N] = one_hot
    lookup[:, N:] = one_hot

    def waves(at, count):
        wave = at + lax.broadcasted_iota(jnp.int32, (1, count), 1)
        wave_x = jnp.abs(wave // (GRID * (GRID // 2)) - GRID // 2).astype(F32)
        wave_z = wave % GRID - GRID // 2
        return wave_x, wave_z >= 0, (jnp.abs(wave_z) * 16).astype(F32)

    def wedge(pick, wave):
        wave_x, upward, need = wave
        limit = jnp.where(upward, chosen[pick, 127:128], chosen[pick, 126:127])
        return jnp.where(need <= limit * wave_x, 1.0, 0.0)

    for side, position in enumerate((r, mate)):
        wave = waves(c * 1024 + position * N, N)
        for source in range(8):
            pick = pl.ds(source * ROWS, ROWS)
            masks[pick, side * N : (side + 1) * N] = wedge(pick, wave)

    own[r] = held[:, :, mine]

    wave = waves(c * 1024, 1024)
    wave_x, upward, need = wave
    own_mask = jnp.concatenate(
        [wedge(rows_at(r * PART, PART), wave), wedge(rows_at(HALF + r * PART, PART), wave)], axis=0
    )
    real, imag = held[0] * own_mask, held[1] * own_mask
    energy = real * real + imag * imag
    slope = lax.broadcasted_iota(jnp.int32, (N, 1), 0)
    below = need <= (slope % 64 + LOW).astype(F32) * wave_x
    side = jnp.where(slope < 64, 1, 0) == jnp.where(upward, 1, 0)
    pattern = jnp.where(below & side, 1.0, 0.0).astype(BF16)
    high = energy.astype(BF16)
    middle, low = split(energy - high.astype(F32))
    sums = nt(high, pattern) + nt(middle, pattern) + nt(low, pattern)

    def ring_send(buffer, value, axis, base):
        buffer[place[axis]] = value
        return [
            send(
                buffer.at[place[axis]], buffer.at[place[axis]],
                tab_s.at[base + d - 1], tab_r.at[base + d - 1], peer(axis, d)[1],
            )
            for d in range(1, 4)
        ]

    copies = ring_send(table_x, sums, "x", 0)
    for copy in starts:
        copy.wait()
    starts = []
    for side in range(2):
        own_rows = rows_at(side * HALF + place["y"] * 2 * PART, 2 * PART)
        for d in range(1, 4):
            n = 3 * side + d + 2
            starts.append(send(first.at[own_rows], first.at[own_rows], st_s.at[n], st_r.at[n], peer("y", d)[1]))
    for copy in copies:
        copy.wait()
    copies = ring_send(table_y, (table_x[0] + table_x[1]) + (table_x[2] + table_x[3]), "y", 3)

    def arrive(step):
        parts, rows = cuts[step]
        for n, (d, copy) in enumerate(exchange[step]):
            copy.wait()
            source = (r - d + 8) % 8
            n = 8 * step + n + 1
            forward[step].append(send(
                own.at[source, parts, rows], other.at[source, parts, rows], fwd_s.at[n], fwd_r.at[n], partner,
            ))
        base = 0 if step == 0 else HALF
        for side, ref in enumerate((own, other)):
            if side == 1:
                for copy in forward[step]:
                    copy.wait()
            lane = slice(side * N, (side + 1) * N)
            for source in range(8):
                pick = pl.ds(base + source * PART, PART)
                mask = masks[pick, lane]
                for part in range(parts.start, parts.stop):
                    high, low = split(ref[source, part, rows, :] * mask)
                    x_high[part, pick, lane] = high
                    x_low[part, pick, lane] = low

    started = {}

    def scatter(s, source, buffer, size, axis, ss, rs):
        copies = []
        for d in range(1, 4):
            p, device = peer(axis, d)
            n = 3 * s + d - 1
            copies.append(send(
                source.at[rows_at(p * size, size)],
                buffer.at[s, d - 1, pl.ds(0, size)], ss.at[n], rs.at[n], device,
            ))
        return copies

    def scatter_a(s):
        at, count, order = STREAMS[s]
        source = partial.at[pl.ds(at * N, count * N)]
        started["a", s] = scatter(s, source, recv_a, count * 32, order[0], ra_s, ra_r)

    def product(J, part):
        odd = (core + J) % 2
        right_high = x_high[part, J * 2 * N : (J + 1) * 2 * N, :]
        right_low = x_low[part, J * 2 * N : (J + 1) * 2 * N, :]
        picks = [pl.ds(pl.multiple_of((2 * i + odd) * N, N), N) for i in range(J + 1)]
        left_high = jnp.concatenate([x_high[part, pick, :] for pick in picks], axis=0)
        left_low = jnp.concatenate([x_low[part, pick, :] for pick in picks], axis=0)
        return nt(left_high, right_high) + nt(left_high, right_low) + nt(left_low, right_high)

    def cut(J, value):
        tiles = [value[i * N : (i + 1) * N, k * N : (k + 1) * N] for i in range(J + 1) for k in range(2)]
        return tiles.pop(2 * J), tiles

    def tile_at(n):
        return slice(n * N, (n + 1) * N)

    def early_products():
        at = 0
        spares = {}
        for J in (2, 1, 0):
            spares[J], tiles = cut(J, product(J, 0) + product(J, 1))
            if J == 0:
                tiles.append(jnp.where(core == 0, spares[0], spares[1]))
            for tile in tiles:
                partial[tile_at(at), :] = tile
                at += 1
        corner[...] = spares[2]
        for s in (0, 1):
            scatter_a(s)

    def late_products(part):
        at = 10
        stream = 2
        spares = {}
        for J in (5, 4, 3):
            spares[J], tiles = cut(J, product(J, part))
            if J == 4:
                tiles.append(jnp.where(core == 0, spares[4], spares[5]))
            if J == 3:
                kept = corner[...] if part == 0 else jnp.zeros((N, N), F32)
                tiles.append(jnp.where(core == 0, kept, spares[3]))
            for tile in tiles:
                if part == 0:
                    partial[tile_at(at), :] = tile
                else:
                    partial[tile_at(at), :] += tile
                at += 1
            while part == 1 and stream < len(STREAMS) and sum(STREAMS[stream][:2]) <= at:
                if stream not in HELD_BACK:
                    scatter_a(stream)
                stream += 1

    def scatter_b(s):
        count, order = STREAMS[s][1:]
        size = count * 32
        for copy in started["a", s]:
            copy.wait()
        pick = rows_at(STREAMS[s][0] * N + place[order[0]] * size, size)
        got = [recv_a[s, n, 0:size, :] for n in range(3)]
        acc[s, 0:size, :] = (partial[pick, :] + got[0]) + (got[1] + got[2])
        started["b", s] = scatter(s, acc.at[s], recv_b, count * 8, order[1], rb_s, rb_r)

    def spread_c(s):
        count, order = STREAMS[s][1:]
        size = count * 8
        for copy in started["b", s]:
            copy.wait()
        got = [recv_b[s, n, 0:size, :] for n in range(3)]
        value = (acc[s, rows_at(place[order[1]] * size, size), :] + got[0]) + (got[1] + got[2])
        here = place[order[2]]
        recv_c[s, here, 0:size, :] = value
        piece = recv_c.at[s, here, pl.ds(0, size)]
        started["c", s] = [
            send(piece, piece, rc_s.at[3 * s + d - 1], rc_r.at[3 * s + d - 1], peer(order[2], d)[1])
            for d in range(1, 4)
        ]

    def gather_b(s):
        at, count, order = STREAMS[s]
        size = count * 8
        for copy in started["c", s]:
            copy.wait()
        got = [recv_c[s, n, 0:size, :] for n in range(4)]
        pick = rows_at(at * N + (place[order[0]] * 4 + place[order[1]]) * size, size)
        full[core, pick, :] = (got[0] + got[1]) + (got[2] + got[3])
        piece = full.at[core, pick]
        started["B", s] = [
            send(piece, piece, gb_s.at[3 * s + d - 1], gb_r.at[3 * s + d - 1], peer(order[1], d)[1])
            for d in range(1, 4)
        ]

    def piece_of(s, d, low, size):
        at, count, order = STREAMS[s]
        seg = (place[order[0]] - d + 4) % 4 * count * 32
        return full.at[core, rows_at(at * N + seg + low, size)]

    def gather_a(s):
        count, order = STREAMS[s][1:]
        for copy in started["B", s]:
            copy.wait()
        piece = piece_of(s, 0, 0, count * 32)
        started["A", s] = {
            d: send(piece, piece, ga_s.at[3 * s + d - 1], ga_r.at[3 * s + d - 1], peer(order[0], d)[1])
            for d in ((1, 3) if s in RELAYED else (1, 3, 2))
        }
        started["out", s] = []
        pass_on(s, 0)

    def pass_on(s, d):
        piece = piece_of(s, d, 0, STREAMS[s][1] * 32)
        started["out", s].append(send(piece, piece, out_s.at[4 * s + d], out_r.at[4 * s + d], partner))

    def relay(s):
        count, order = STREAMS[s][1:]
        halves = []
        for d, low in ((1, 0), (3, count * 16)):
            started["A", s][d].wait()
            piece = piece_of(s, d, low, count * 16)
            n = 3 * s + 1 if d == 1 else 33 + s
            halves.append(send(piece, piece, ga_s.at[n], ga_r.at[n], peer(order[0], d)[1]))
            pass_on(s, d)
        started["H", s] = halves

    def finish(s):
        if s in RELAYED:
            for copy in started["H", s]:
                copy.wait()
            pass_on(s, 2)
        else:
            for d in (1, 3, 2):
                started["A", s][d].wait()
                pass_on(s, d)

    def assemble(s):
        at, count, order = STREAMS[s]
        for copy in started["out", s]:
            copy.wait()
        for tile in range(at, at + count):
            for half in range(2):
                A, B = SLOTS[half][tile]
                pick = slice(tile * N, (tile + 1) * N)
                value = full[half, pick, :] * rden[half, pick, :]
                high, low = split(value)
                down, across = slice(A * N, (A + 1) * N), slice(B * N, (B + 1) * N)
                c_high[down, across] = high
                c_low[down, across] = low
                if A < B:
                    high, low = split(value.T)
                    c_high[across, down] = high
                    c_low[across, down] = low

    arrive(0)
    early_products()
    arrive(1)
    late_products(0)
    for copy in copies:
        copy.wait()
    table[r] = (table_y[0] + table_y[1]) + (table_y[2] + table_y[3])
    copies = [
        send(table.at[r], table.at[r], tab_s.at[5 + d], tab_r.at[5 + d], peer("z", d)[1])
        for d in range(1, 4)
    ]
    table_forward = [send(table.at[r], table.at[r], tf_s.at[0], tf_r.at[0], partner)]
    for copy in starts:
        copy.wait()
    arrive(2)
    for s in (0, 1):
        scatter_b(s)
    late_products(1)

    def table_pass(_):
        for d, copy in zip(range(1, 4), copies):
            copy.wait()
            source = ((place["z"] - d + 4) % 4) * 2 + core
            table_forward.append(send(table.at[source], table.at[source], tf_s.at[d], tf_r.at[d], partner))

    def table_done(_):
        for copy in table_forward:
            copy.wait()
        for source in range(8):
            for side in range(2):
                high, low = split(table[source, side * PART : (side + 1) * PART, :])
                at = side * HALF + source * PART
                lookup_in[at : at + PART, 0:N] = high
                lookup_in[at : at + PART, N:] = low

    def norms(item):
        half, J = item
        odd = (half + J) % 2
        right = slice(J * 2 * N, (J + 1) * 2 * N)
        picks = [tile_at(2 * i + odd) for i in range(J + 1)]
        sums_in = jnp.concatenate([lookup_in[pick, :] for pick in picks], axis=0)
        select = jnp.concatenate([lookup[pick, :] for pick in picks], axis=0)
        value = lax.rsqrt(nt(sums_in, lookup[right, :]) * nt(select, lookup_in[right, :]) + EPS)
        for i in range(J + 1):
            for k in range(2):
                tile = (2 * i + odd, 2 * J + k)
                if tile in PLACE[half]:
                    at = PLACE[half][tile]
                    rden[half, tile_at(at), :] = value[i * N : (i + 1) * N, k * N : (k + 1) * N]

    tasks = [(3.2, table_pass, 0), (4.6, table_done, 0)]
    for n, J in enumerate((2, 1, 0, 5, 4, 3)):
        tasks += [(5.3 + n, norms, (0, J)), (5.8 + n, norms, (1, J))]
    for s, start_at in zip((0, 1), (0.0, 0.1)):
        tasks += [(1.7 + start_at, spread_c, s), (6.2 + start_at, gather_b, s), (11.5 + start_at, gather_a, s)]
        if s in RELAYED:
            tasks += [(19.0 + start_at, relay, s)]
        tasks += [(21.8 + start_at, finish, s), (22.2 + start_at, assemble, s)]
    for n, s in enumerate(HELD_BACK):
        tasks.append((1.9 + n * 0.01, scatter_a, s))
    for s in range(2, len(STREAMS)):
        chunk = (s - 2) // 3
        start_at = 2.2 * chunk + 0.01 * s + (0.8 if s in HELD_BACK else 0.0)
        tasks += [(3.5 + start_at, scatter_b, s), (7.4 + start_at, spread_c, s)]
        tasks += [(11.3 + start_at, gather_b, s)]
        start_at = 2.2 * chunk + 0.01 * s
        if s in RELAYED:
            tasks += [(17.2 + start_at, gather_a, s), (21.0 + start_at, relay, s)]
            tasks += [(25.8 + start_at, finish, s), (26.0 + start_at, assemble, s)]
        else:
            tasks += [(19.6 + start_at, gather_a, s), (26 + start_at, finish, s), (26.5 + start_at, assemble, s)]
    for start_at, task, s in sorted(tasks, key=lambda item: item[0]):
        task(s)

    def times_matrix(high, low):
        wide = nn(jnp.concatenate([high, low], axis=0), c_high[...])
        return wide[0:32] + wide[32:64] + nn(high, c_low[...])

    def gram_of(high, low):
        return nt(high, high) + (nt(high, low) + nt(low, high))

    def solved(inverse, high, low):
        inverse_high, inverse_low = split(inverse)
        return nn(inverse_high, high) + (nn(inverse_high, low) + nn(inverse_low, high))

    wt[...] = first[...].T[0:32, :]

    def iterate(step, carry):
        high, low = split(times_matrix(*split(wt[...])))
        inverse = lower_inverse(gram_of(high, low))
        wt[...] = solved(inverse, high, low)
        return carry

    lax.fori_loop(0, ITERS, iterate, 0)
    first[:, 0:32] = (wt[...] * math.sqrt(1536)).T
    basis_out[...] = first[rows_at(here, PART), :].T[0:32, :]
    lane = jnp.minimum(here // N, 1536 // N - 2) * N
    window = pl.ds(pl.multiple_of(lane, N), 2 * N)
    shift = (2 * N - (here - lane)) % (2 * N)
    for side in range(2):
        pick = pl.ds(pl.multiple_of(side * HALF + r * PART, 16), PART)
        block = c_high[pick, window].astype(F32) + c_low[pick, window].astype(F32)
        block_out[side * PART : (side + 1) * PART, :] = pltpu.roll(block, shift, 1)[:, 0:PART]


def local(coefs, tilts, start_basis):
    vmem = pl.BlockSpec(memory_space=pltpu.VMEM)
    dma = pltpu.SemaphoreType.DMA
    block, basis = pl.pallas_call(
        kernel,
        out_shape=(
            pltpu.VMEM((ROWS, PART), F32),
            pltpu.VMEM((32, PART), F32),
        ),
        in_specs=[pl.BlockSpec(memory_space=pltpu.HBM)] * 3,
        out_specs=(vmem, vmem),
        scratch_shapes=[
            pltpu.VMEM((2, 1536), jnp.int32),
            pltpu.VMEM((32, PART), F32),
            pltpu.VMEM((2, ROWS, 1024), F32),
            pltpu.VMEM((8, 2, ROWS, N), F32),
            pltpu.VMEM((8, 2, ROWS, N), F32),
            pltpu.VMEM((2, 1536, 2 * N), BF16),
            pltpu.VMEM((2, 1536, 2 * N), BF16),
            pltpu.VMEM((1536, 2 * N), F32),
            pltpu.VMEM((1536, N), F32),
            pltpu.VMEM((N, N), F32),
            pltpu.VMEM((TILES * N, N), F32),
            pltpu.VMEM((11, 3, MOST * 32, N), F32),
            pltpu.VMEM((11, 3, MOST * 8, N), F32),
            pltpu.VMEM((11, 4, MOST * 8, N), F32),
            pltpu.VMEM((11, MOST * 32, N), F32),
            pltpu.VMEM((2, TILES * N, N), F32),
            pltpu.VMEM((2, TILES * N, N), F32),
            pltpu.VMEM((4, ROWS, N), F32),
            pltpu.VMEM((4, ROWS, N), F32),
            pltpu.VMEM((8, ROWS, N), F32),
            pltpu.VMEM((1536, 2 * N), BF16),
            pltpu.VMEM((1536, 2 * N), BF16),
            pltpu.VMEM((1536, N), F32),
            pltpu.VMEM((1536, 1536), BF16),
            pltpu.VMEM((1536, 1536), BF16),
            pltpu.VMEM((32, 1536), F32),
            dma((3,)),
            dma((21,)), dma((21,)), dma((24,)), dma((24,)),
            dma((9,)), dma((9,)), dma((4,)), dma((4,)), dma((9,)), dma((9,)),
            dma((33,)), dma((33,)), dma((33,)), dma((33,)), dma((33,)), dma((33,)),
            dma((33,)), dma((33,)), dma((44,)), dma((44,)), dma((44,)), dma((44,)),
        ],
        compiler_params=pltpu.CompilerParams(
            collective_id=0, has_side_effects=True, vmem_limit_bytes=55296 << 10
        ),
        name="whole",
    )(coefs, tilts.T, start_basis.T)
    return block, basis.T


def solution(mesh):
    in_specs = (P(None, "row", "col"), P(), P("col", None))
    out_specs = (P("row", "col"), P("col", None))
    return jax.shard_map(local, mesh=mesh, in_specs=in_specs, out_specs=out_specs, check_vma=False)
```

time: 85.3 us -> 83.4 us (0.978)
  local copies, waits for them, and re-layouts: 2.66 us -> 1.25 us
    unnamed x6 -> x2, local copies, waits for them, and re-layouts: 2.66 us -> 1.25 us
where the time goes in v3:
time: 83.4 us; the launch traced here: 83.2 us
  Pallas kernels  81.3 us (97%)
  local copies, waits for them, and re-layouts  1.25 us (1%)
    pallas_call x1, Pallas kernels, local(): pl.pallas_call(kernel, out_shape=(pltpu.VMEM((ROWS, PART), F32), pltpu.VM...  81.3 us

profile of v3, /device:TPU:1, one launch (start us, length us, event | category | flops | bytes accessed | tf_op | source)
XLA Modules:
  0.0 83.2 jit_solution(12344843058176738719)
XLA Ops:
  0.6 81.3 %whole.1 = (f32[192,96]{1,0:T(8,128)S(1)}, f32[32,96]{1,0:T(8,128)S(1)}) custom-call(f32[2,192,1024]{2,1,0:T(8,128)} %coefs.1, s32[2,1536]{1,0:T(2,128)} %bitcast.5, f32[32,96]{1,0:T(8,128)} %bitcast.4), custom_call_target="tpu_custom_call" | custom-call | tf_op jit(solution)/shard_map/whole/pallas_call | solution.py:545
  82.0 0.6 copy.7
  82.6 0.6 copy.8

commit v4 on v3

--- a/solution.py
+++ b/solution.py
@@ -13,6 +13,7 @@
 MESH = pl.DeviceIdType.MESH
 F32 = jnp.float32
 BF16 = jnp.bfloat16
+F8 = jnp.float8_e4m3fn
 
 ROWS = 192
 PART = 96
@@ -92,7 +93,7 @@
     tilts, start, held, own, other, x_high, x_low, masks, chosen, corner,
     partial, recv_a, recv_b, recv_c, acc, full, rden,
     table_x, table_y, table, lookup, lookup_in, first,
-    c_high, c_low, wt,
+    c_high, c_low, grow, wt,
     held_s, a2a_s, a2a_r, fwd_s, fwd_r, tab_s, tab_r, tf_s, tf_r, st_s, st_r,
     ra_s, ra_r, rb_s, rb_r, rc_s, rc_r, gb_s, gb_r, ga_s, ga_r, out_s, out_r,
 ):
@@ -425,14 +426,14 @@
                 A, B = SLOTS[half][tile]
                 pick = slice(tile * N, (tile + 1) * N)
                 value = full[half, pick, :] * rden[half, pick, :]
-                high, low = split(value)
+                high = value.astype(BF16)
+                low = (value - high.astype(F32)) * grow[0:1, :]
                 down, across = slice(A * N, (A + 1) * N), slice(B * N, (B + 1) * N)
                 c_high[down, across] = high
-                c_low[down, across] = low
+                c_low[down, across] = low.astype(F8)
                 if A < B:
-                    high, low = split(value.T)
-                    c_high[across, down] = high
-                    c_low[across, down] = low
+                    c_high[across, down] = value.T.astype(BF16)
+                    c_low[across, down] = low.T.astype(F8)
 
     arrive(0)
     early_products()
@@ -468,6 +469,10 @@
                 at = side * HALF + source * PART
                 lookup_in[at : at + PART, 0:N] = high
                 lookup_in[at : at + PART, N:] = low
+        most = jnp.max(jnp.max(table[...], axis=0), axis=0, keepdims=True)
+        most = 2.0 * jnp.max(most, axis=1, keepdims=True)
+        factor = 65536.0 * jnp.sqrt(most * most + EPS) / jnp.maximum(most, 1e-30)
+        grow[...] = jnp.broadcast_to(factor, (8, N))
 
     def norms(item):
         half, J = item
@@ -510,7 +515,7 @@
 
     def times_matrix(high, low):
         wide = nn(jnp.concatenate([high, low], axis=0), c_high[...])
-        return wide[0:32] + wide[32:64] + nn(high, c_low[...])
+        return wide[0:32] + (wide[32:64] + nn(high, c_low[...]) * (1.0 / grow[0:1, 0:1]))
 
     def gram_of(high, low):
         return nt(high, high) + (nt(high, low) + nt(low, high))
@@ -534,8 +539,8 @@
     window = pl.ds(pl.multiple_of(lane, N), 2 * N)
     shift = (2 * N - (here - lane)) % (2 * N)
     for side in range(2):
-        pick = pl.ds(pl.multiple_of(side * HALF + r * PART, 16), PART)
-        block = c_high[pick, window].astype(F32) + c_low[pick, window].astype(F32)
+        pick = pl.ds(pl.multiple_of(side * HALF + r * PART, 32), PART)
+        block = c_high[pick, window].astype(F32) + c_low[pick, window].astype(F32) * (1.0 / grow[0:1, 0:1])
         block_out[side * PART : (side + 1) * PART, :] = pltpu.roll(block, shift, 1)[:, 0:PART]
 
 
@@ -575,7 +580,8 @@
             pltpu.VMEM((1536, 2 * N), BF16),
             pltpu.VMEM((1536, N), F32),
             pltpu.VMEM((1536, 1536), BF16),
-            pltpu.VMEM((1536, 1536), BF16),
+            pltpu.VMEM((1536, 1536), F8),
+            pltpu.VMEM((8, N), F32),
             pltpu.VMEM((32, 1536), F32),
             dma((3,)),
             dma((21,)), dma((21,)), dma((24,)), dma((24,)),

time: 83.4 us -> 81.7 us (0.980)
  Pallas kernels: 81.3 us -> 79.6 us
    pallas_call x1, Pallas kernels: 81.3 us -> 79.6 us  [local(): pl.pallas_call(kernel, out_shape=(pltpu.VMEM((ROWS, PART), F32), pltpu.VM...]
where the time goes in v4:
time: 81.7 us; the launch traced here: 81.5 us
  Pallas kernels  79.6 us (97%)
  local copies, waits for them, and re-layouts  1.25 us (2%)
    pallas_call x1, Pallas kernels, local(): pl.pallas_call(kernel, out_shape=(pltpu.VMEM((ROWS, PART), F32), pltpu.VM...  79.6 us

profile of v4, /device:TPU:1, one launch (start us, length us, event | category | flops | bytes accessed | tf_op | source)
XLA Modules:
  0.0 81.5 jit_solution(7323130212372407104)
XLA Ops:
  0.6 79.6 %whole.1 = (f32[192,96]{1,0:T(8,128)S(1)}, f32[32,96]{1,0:T(8,128)S(1)}) custom-call(f32[2,192,1024]{2,1,0:T(8,128)} %coefs.1, s32[2,1536]{1,0:T(2,128)} %bitcast.5, f32[32,96]{1,0:T(8,128)} %bitcast.4), custom_call_target="tpu_custom_call" | custom-call | tf_op jit(solution)/shard_map/whole/pallas_call | solution.py:550
  80.3 0.6 copy.7
  80.9 0.6 copy.8

commit v5 on v4

--- a/solution.py
+++ b/solution.py
@@ -432,8 +432,8 @@
                 c_high[down, across] = high
                 c_low[down, across] = low.astype(F8)
                 if A < B:
-                    c_high[across, down] = value.T.astype(BF16)
-                    c_low[across, down] = low.T.astype(F8)
+                    c_high[across, down] = high.T
+                    c_low[across, down] = low.astype(BF16).T.astype(F8)
 
     arrive(0)
     early_products()
@@ -496,7 +496,7 @@
         tasks += [(1.7 + start_at, spread_c, s), (6.2 + start_at, gather_b, s), (11.5 + start_at, gather_a, s)]
         if s in RELAYED:
             tasks += [(19.0 + start_at, relay, s)]
-        tasks += [(21.8 + start_at, finish, s), (22.2 + start_at, assemble, s)]
+        tasks += [(21.8 + start_at, finish, s), (26.2 + start_at, assemble, s)]
     for n, s in enumerate(HELD_BACK):
         tasks.append((1.9 + n * 0.01, scatter_a, s))
     for s in range(2, len(STREAMS)):
@@ -509,7 +509,7 @@
             tasks += [(17.2 + start_at, gather_a, s), (21.0 + start_at, relay, s)]
             tasks += [(25.8 + start_at, finish, s), (26.0 + start_at, assemble, s)]
         else:
-            tasks += [(19.6 + start_at, gather_a, s), (26 + start_at, finish, s), (26.5 + start_at, assemble, s)]
+            tasks += [(19.6 + start_at, gather_a, s), (26 + start_at, finish, s), (28.4 + start_at, assemble, s)]
     for start_at, task, s in sorted(tasks, key=lambda item: item[0]):
         task(s)
 

time: 81.7 us -> 80.6 us (0.987)
  Pallas kernels: 79.6 us -> 78.6 us
    pallas_call x1, Pallas kernels: 79.6 us -> 78.6 us  [local(): pl.pallas_call(kernel, out_shape=(pltpu.VMEM((ROWS, PART), F32), pltpu.VM...]
where the time goes in v5:
time: 80.6 us; the launch traced here: 80.4 us
  Pallas kernels  78.6 us (98%)
  local copies, waits for them, and re-layouts  1.25 us (2%)
    pallas_call x1, Pallas kernels, local(): pl.pallas_call(kernel, out_shape=(pltpu.VMEM((ROWS, PART), F32), pltpu.VM...  78.6 us

profile of v5, /device:TPU:1, one launch (start us, length us, event | category | flops | bytes accessed | tf_op | source)
XLA Modules:
  0.0 80.4 jit_solution(4538800755353835214)
XLA Ops:
  0.6 78.6 %whole.1 = (f32[192,96]{1,0:T(8,128)S(1)}, f32[32,96]{1,0:T(8,128)S(1)}) custom-call(f32[2,192,1024]{2,1,0:T(8,128)} %coefs.1, s32[2,1536]{1,0:T(2,128)} %bitcast.5, f32[32,96]{1,0:T(8,128)} %bitcast.4), custom_call_target="tpu_custom_call" | custom-call | tf_op jit(solution)/shard_map/whole/pallas_call | solution.py:550
  79.2 0.6 copy.7
  79.8 0.6 copy.8

commit v6 on v5

--- a/solution.py
+++ b/solution.py
@@ -493,7 +493,7 @@
     for n, J in enumerate((2, 1, 0, 5, 4, 3)):
         tasks += [(5.3 + n, norms, (0, J)), (5.8 + n, norms, (1, J))]
     for s, start_at in zip((0, 1), (0.0, 0.1)):
-        tasks += [(1.7 + start_at, spread_c, s), (6.2 + start_at, gather_b, s), (11.5 + start_at, gather_a, s)]
+        tasks += [(1.7 + start_at, spread_c, s), (6.2 + start_at, gather_b, s), (10.5 + start_at, gather_a, s)]
         if s in RELAYED:
             tasks += [(19.0 + start_at, relay, s)]
         tasks += [(21.8 + start_at, finish, s), (26.2 + start_at, assemble, s)]

time: 80.6 us -> 80.2 us (level)
  no operation moved by 1% of the time
where the time goes in v6:
time: 80.2 us; the launch traced here: 80.1 us
  Pallas kernels  78.2 us (98%)
  local copies, waits for them, and re-layouts  1.25 us (2%)
    pallas_call x1, Pallas kernels, local(): pl.pallas_call(kernel, out_shape=(pltpu.VMEM((ROWS, PART), F32), pltpu.VM...  78.2 us

profile of v6, /device:TPU:1, one launch (start us, length us, event | category | flops | bytes accessed | tf_op | source)
XLA Modules:
  0.0 80.1 jit_solution(6250218243874196121)
XLA Ops:
  0.6 78.2 %whole.1 = (f32[192,96]{1,0:T(8,128)S(1)}, f32[32,96]{1,0:T(8,128)S(1)}) custom-call(f32[2,192,1024]{2,1,0:T(8,128)} %coefs.1, s32[2,1536]{1,0:T(2,128)} %bitcast.5, f32[32,96]{1,0:T(8,128)} %bitcast.4), custom_call_target="tpu_custom_call" | custom-call | tf_op jit(solution)/shard_map/whole/pallas_call | solution.py:550
  78.8 0.6 copy.7
  79.5 0.6 copy.8

commit v7 on v6

--- a/solution.py
+++ b/solution.py
@@ -509,7 +509,7 @@
             tasks += [(17.2 + start_at, gather_a, s), (21.0 + start_at, relay, s)]
             tasks += [(25.8 + start_at, finish, s), (26.0 + start_at, assemble, s)]
         else:
-            tasks += [(19.6 + start_at, gather_a, s), (26 + start_at, finish, s), (28.4 + start_at, assemble, s)]
+            tasks += [((15.7, 21.8, 24.0)[chunk] + 0.01 * s, gather_a, s), (26 + start_at, finish, s), (28.4 + start_at, assemble, s)]
     for start_at, task, s in sorted(tasks, key=lambda item: item[0]):
         task(s)
 

time: 80.2 us -> 81.2 us (1.012)
  Pallas kernels: 78.2 us -> 79.2 us
    pallas_call x1, Pallas kernels: 78.2 us -> 79.2 us  [local(): pl.pallas_call(kernel, out_shape=(pltpu.VMEM((ROWS, PART), F32), pltpu.VM...]
where the time goes in v7:
time: 81.2 us; the launch traced here: 81.1 us
  Pallas kernels  79.2 us (98%)
  local copies, waits for them, and re-layouts  1.25 us (2%)
    pallas_call x1, Pallas kernels, local(): pl.pallas_call(kernel, out_shape=(pltpu.VMEM((ROWS, PART), F32), pltpu.VM...  79.2 us

profile of v7, /device:TPU:1, one launch (start us, length us, event | category | flops | bytes accessed | tf_op | source)
XLA Modules:
  0.0 81.1 jit_solution(3145365407911851087)
XLA Ops:
  0.6 79.2 %whole.1 = (f32[192,96]{1,0:T(8,128)S(1)}, f32[32,96]{1,0:T(8,128)S(1)}) custom-call(f32[2,192,1024]{2,1,0:T(8,128)} %coefs.1, s32[2,1536]{1,0:T(2,128)} %bitcast.5, f32[32,96]{1,0:T(8,128)} %bitcast.4), custom_call_target="tpu_custom_call" | custom-call | tf_op jit(solution)/shard_map/whole/pallas_call | solution.py:550
  79.8 0.6 copy.7
  80.5 0.6 copy.8
